TPU v7x, 32 devices: a whole 2x2x4 slice. The times are simulated.
32 devices in a mesh: px: 8 (over z, x), py: 4 (over y, core).
Axes of the slice: x: 2, y: 2, z: 4, core: 2. Of those that a mesh axis runs over, the one named last changes fastest.
Arguments:
- potential: float32 [256, 256, 256], P(('px', 'py')), may hold values from 0 to 1
- recovery: float32 [256, 256, 256], P(('px', 'py')), may hold values from 0 to 2
- stimulus: float32 [256, 256, 256], P(('px', 'py')), may hold values from -8 to 8
- conductivity: float32 [256, 256, 256], P('px', 'py'), may hold values from 0.2 to 5
Outputs:
- potential_next: float32 [256, 256, 256], P(('px', 'py'))
- recovery_next: float32 [256, 256, 256], P(('px', 'py'))
All inputs are finite; a program needn't handle non-finite values.
Results may differ from a plain program's by a relative error of at most 0.0003.
Values sent between devices are 32-bit elements; how exact they have to be, the bound alone decides.
No kernel may reach another device: no remote copies, remote signals or barrier semaphores. Data moves between devices by JAX's collectives and lax.ppermute only.
A program may use at most 128 MiB of HBM per device.

v0:
```python
import math

import jax
import jax.numpy as jnp
from jax import lax
from jax.sharding import PartitionSpec as P

GX = 256
GY = 256
GZ = 256
ITERS = 4


mass_rate = 0.01
mean_conduct = 1.0
excite_gain = 8.0
threshold = 0.15
base_rate = 0.002
rate_slope = 0.2
rate_shift = 0.3
time_step = 0.1
forms = ("xyz,xk->kyz", "xyz,yk->xkz", "xyz,zk->xyk")


def padded_2(cells, sides, width):
    for axis, dim in sides:
        count = lax.axis_size(axis)
        head = lax.slice_in_dim(cells, 0, width, axis=dim)
        tail = lax.slice_in_dim(cells, cells.shape[dim] - width, cells.shape[dim], axis=dim)
        cells = jnp.concatenate(
            [
                lax.ppermute(tail, axis, [(i, (i + 1) % count) for i in range(count)]),
                cells,
                lax.ppermute(head, axis, [((i + 1) % count, i) for i in range(count)]),
            ],
            axis=dim,
        )
    return cells


def dft_tables(length):
    steps = jnp.arange(length, dtype=jnp.int32)
    phase = steps[:, None] * steps[None, :] % length
    angle = 2.0 * math.pi / length * phase.astype(jnp.float32)
    return (jnp.cos(angle), jnp.sin(angle))


def cas_table(length):
    cosine, sine = dft_tables(length)
    return cosine + sine


def along(field, table, dimension):
    return jnp.einsum(forms[dimension], field, table, precision=lax.Precision.HIGHEST)


def wave_term(length, start, count):
    modes = start + jnp.arange(count, dtype=jnp.int32)
    return 2.0 - 2.0 * jnp.cos(2.0 * math.pi / length * modes.astype(jnp.float32))


def precondition_cas(residual, x_cas, y_cas, z_cas):
    spectrum = along(residual, z_cas, 2)
    spectrum = along(
        lax.all_to_all(spectrum, "py", split_axis=2, concat_axis=1, tiled=True), y_cas, 1
    )
    spectrum = along(
        lax.all_to_all(spectrum, "px", split_axis=1, concat_axis=0, tiled=True), x_cas, 0
    )
    count_y = spectrum.shape[1]
    count_z = spectrum.shape[2]
    symbol = mass_rate + mean_conduct * (
        wave_term(GX, 0, GX)[:, None, None]
        + wave_term(GY, lax.axis_index("px") * count_y, count_y)[None, :, None]
        + wave_term(GZ, lax.axis_index("py") * count_z, count_z)[None, None, :]
    )
    spectrum = along(spectrum / symbol, x_cas, 0) * (1.0 / GX)
    spectrum = along(
        lax.all_to_all(spectrum, "px", split_axis=0, concat_axis=1, tiled=True), y_cas, 1
    ) * (1.0 / GY)
    return along(
        lax.all_to_all(spectrum, "py", split_axis=1, concat_axis=2, tiled=True), z_cas, 2
    ) * (1.0 / GZ)


def local(potential, recovery, stimulus, conductivity):
    drive = (
        excite_gain * potential * (potential - threshold) * (1.0 - potential) - potential * recovery
    )
    v_star = potential + time_step * (drive + stimulus)
    rate = base_rate + rate_slope * recovery / (potential + rate_shift)
    recovery_next = recovery + time_step * rate * (
        -recovery - excite_gain * potential * (potential - threshold - 1.0)
    )
    start_field = lax.all_to_all(v_star, "py", split_axis=1, concat_axis=0, tiled=True)
    cond_pad = padded_2(conductivity, (("px", 0), ("py", 1)), 1)
    face_xplus = 0.5 * (conductivity + cond_pad[2:, 1:-1])
    face_xminus = 0.5 * (conductivity + cond_pad[:-2, 1:-1])
    face_yplus = 0.5 * (conductivity + cond_pad[1:-1, 2:])
    face_yminus = 0.5 * (conductivity + cond_pad[1:-1, :-2])
    face_zplus = 0.5 * (conductivity + jnp.roll(conductivity, -1, 2))
    face_zminus = 0.5 * (conductivity + jnp.roll(conductivity, 1, 2))

    def operate(field):
        padded = padded_2(field, (("px", 0), ("py", 1)), 1)
        result_sum = mass_rate * field
        result_sum = (
            result_sum
            + face_xplus * (field - padded[2:, 1:-1])
            + face_xminus * (field - padded[:-2, 1:-1])
        )
        result_sum = (
            result_sum
            + face_yplus * (field - padded[1:-1, 2:])
            + face_yminus * (field - padded[1:-1, :-2])
        )
        result_sum = (
            result_sum
            + face_zplus * (field - jnp.roll(field, -1, 2))
            + face_zminus * (field - jnp.roll(field, 1, 2))
        )
        return result_sum

    x_cas = cas_table(GX)
    y_cas = cas_table(GY)
    z_cas = cas_table(GZ)

    def apply_inverse(residual):
        return precondition_cas(residual, x_cas, y_cas, z_cas)

    solution = start_field
    residual = mass_rate * start_field - operate(solution)

    def product_sum(residual, precond):
        return lax.psum(jnp.sum(residual * precond), ("px", "py"))

    precond = apply_inverse(residual)
    direction = precond
    product_now = product_sum(residual, precond)
    for step in range(ITERS):
        image = operate(direction)
        alpha = product_now / lax.psum(jnp.sum(direction * image), ("px", "py"))
        solution = solution + alpha * direction
        residual = residual - alpha * image
        if step < ITERS - 1:
            precond = apply_inverse(residual)
            product_next = product_sum(residual, precond)
            direction = precond + product_next / product_now * direction
            product_now = product_next
    potential_next = lax.all_to_all(solution, "py", split_axis=0, concat_axis=1, tiled=True)
    return (potential_next, recovery_next)


def solution(mesh):
    in_specs = (
        P(("px", "py"), None, None),
        P(("px", "py"), None, None),
        P(("px", "py"), None, None),
        P("px", "py", None),
    )
    out_specs = (P(("px", "py"), None, None), P(("px", "py"), None, None))
    return jax.shard_map(local, mesh=mesh, in_specs=in_specs, out_specs=out_specs, check_vma=False)
```

profile of v0, /device:TPU:0, one launch (start us, length us, event | category | flops | bytes accessed | tf_op | source)
XLA Modules:
  0.0 1881.2 jit_solution(16625585675331391221)
XLA Ops:
  0.6 9.3 multiply_add_fusion
  28.2 13.1 all-to-all-done
  55.5 14.4 fusion.63
  86.4 30.3 %all_to_all.324 = f32[4,1,131072]{2,1,0:T(1,128)} all-to-all(f32[4,1,131072]{2,1,0:T(1,128)} %reshape.95), channel_id=1, replica_groups=mesh['px'=8,'py'=4] {'py'}, dimensions={0} | all-to-all | bytes 4194304 | tf_op jit(solution)/shard_map/all_to_all | solution.py:65
  117.2 8.9 reduce
  131.6 6.9 copy.137
  155.5 7.2 reshape.97
  168.6 47.7 %all-to-all-done.2 = f32[8,1,65536]{2,1,0:T(1,128)} async-done(((f32[8,1,65536]{2,1,0:T(1,128)}), f32[8,1,65536]{2,1,0:T(1,128)}, u32[]{:S(2)}, u32[]{:S(2)}) %all-to-all-start.2) | async-done | bytes 2097184 | tf_op jit(solution)/shard_map/all_to_all | solution.py:68
  216.3 8.4 reduce.1
  256.3 7.2 reshape.99
  263.5 52.7 %all_to_all.325 = f32[8,1,65536]{2,1,0:T(1,128)} all-to-all(f32[8,1,65536]{2,1,0:T(1,128)} %reshape.99), channel_id=1, replica_groups=mesh['px'=8,'py'=4] {'px'}, dimensions={0} | all-to-all | bytes 4194304 | tf_op jit(solution)/shard_map/all_to_all | solution.py:79
  316.2 8.4 reduce.2
  355.6 30.1 %all_to_all.326 = f32[4,1,131072]{2,1,0:T(1,128)} all-to-all(f32[4,1,131072]{2,1,0:T(1,128)} %reshape.101), channel_id=1, replica_groups=mesh['px'=8,'py'=4] {'py'}, dimensions={0} | all-to-all | bytes 4194304 | tf_op jit(solution)/shard_map/all_to_all | solution.py:82
  385.7 8.9 reduce.3
  400.1 6.9 copy.136
  429.6 9.3 multiply_reduce_fusion.5
  438.9 38.9 %all-reduce = (f32[]{:T(128)}, f32[]{:T(128)}) all-reduce(f32[]{:T(128)} %get-tuple-element.5, f32[]{:T(128)} %get-tuple-element.4), channel_id=1, replica_groups=mesh['px'=8,'py'=4] {'px','py'}, use_global_device_ids=true, to_apply=%region_1.2 | all-reduce | flops 2 | bytes 16 | tf_op jit(solution)/shard_map/psum | solution.py:135
  498.2 30.3 %all_to_all.327 = f32[4,1,131072]{2,1,0:T(1,128)} all-to-all(f32[4,1,131072]{2,1,0:T(1,128)} %reshape.103), channel_id=1, replica_groups=mesh['px'=8,'py'=4] {'py'}, dimensions={0} | all-to-all | bytes 4194304 | tf_op jit(solution)/shard_map/all_to_all | solution.py:65
  528.5 8.9 reduce.4
  542.9 6.9 copy.135
  566.6 7.2 reshape.105
  573.8 54.2 %all_to_all.328 = f32[8,1,65536]{2,1,0:T(1,128)} all-to-all(f32[8,1,65536]{2,1,0:T(1,128)} %reshape.105), channel_id=1, replica_groups=mesh['px'=8,'py'=4] {'px'}, dimensions={0} | all-to-all | bytes 4194304 | tf_op jit(solution)/shard_map/all_to_all | solution.py:68
  628.0 8.4 reduce.5
  668.3 7.2 reshape.107
  675.5 52.0 %all_to_all.329 = f32[8,1,65536]{2,1,0:T(1,128)} all-to-all(f32[8,1,65536]{2,1,0:T(1,128)} %reshape.107), channel_id=1, replica_groups=mesh['px'=8,'py'=4] {'px'}, dimensions={0} | all-to-all | bytes 4194304 | tf_op jit(solution)/shard_map/all_to_all | solution.py:79
  727.4 8.4 reduce.6
  767.2 30.1 %all_to_all.330 = f32[4,1,131072]{2,1,0:T(1,128)} all-to-all(f32[4,1,131072]{2,1,0:T(1,128)} %reshape.109), channel_id=1, replica_groups=mesh['px'=8,'py'=4] {'py'}, dimensions={0} | all-to-all | bytes 4194304 | tf_op jit(solution)/shard_map/all_to_all | solution.py:82
  797.3 8.9 reduce.7
  811.7 6.9 copy.134
  824.0 7.1 multiply_reduce_fusion.4
  831.1 38.9 %psum.58 = f32[]{:T(128)} all-reduce(f32[]{:T(128)} %get-tuple-element.70), channel_id=1, replica_groups=mesh['px'=8,'py'=4] {'px','py'}, use_global_device_ids=true, to_apply=%region_5.6 | all-reduce | flops 1 | bytes 8 | tf_op jit(solution)/shard_map/psum | solution.py:135
  891.9 40.2 %psum.59 = f32[]{:T(128)} all-reduce(f32[]{:T(128)} %get-tuple-element.10), channel_id=1, replica_groups=mesh['px'=8,'py'=4] {'px','py'}, use_global_device_ids=true, to_apply=%region_7.8 | all-reduce | flops 1 | bytes 8 | tf_op jit(solution)/shard_map/psum | solution.py:142
  952.5 30.3 %all_to_all.331 = f32[4,1,131072]{2,1,0:T(1,128)} all-to-all(f32[4,1,131072]{2,1,0:T(1,128)} %reshape.111), channel_id=1, replica_groups=mesh['px'=8,'py'=4] {'py'}, dimensions={0} | all-to-all | bytes 4194304 | tf_op jit(solution)/shard_map/all_to_all | solution.py:65
  982.9 8.9 reduce.8
  997.3 6.9 copy.133
  1021.2 7.2 reshape.113
  1028.3 54.2 %all_to_all.332 = f32[8,1,65536]{2,1,0:T(1,128)} all-to-all(f32[8,1,65536]{2,1,0:T(1,128)} %reshape.113), channel_id=1, replica_groups=mesh['px'=8,'py'=4] {'px'}, dimensions={0} | all-to-all | bytes 4194304 | tf_op jit(solution)/shard_map/all_to_all | solution.py:68
  1082.5 8.4 reduce.9
  1122.6 7.2 reshape.115
  1129.7 52.2 %all_to_all.333 = f32[8,1,65536]{2,1,0:T(1,128)} all-to-all(f32[8,1,65536]{2,1,0:T(1,128)} %reshape.115), channel_id=1, replica_groups=mesh['px'=8,'py'=4] {'px'}, dimensions={0} | all-to-all | bytes 4194304 | tf_op jit(solution)/shard_map/all_to_all | solution.py:79
  1181.9 8.4 reduce.10
  1221.5 30.1 %all_to_all.334 = f32[4,1,131072]{2,1,0:T(1,128)} all-to-all(f32[4,1,131072]{2,1,0:T(1,128)} %reshape.117), channel_id=1, replica_groups=mesh['px'=8,'py'=4] {'py'}, dimensions={0} | all-to-all | bytes 4194304 | tf_op jit(solution)/shard_map/all_to_all | solution.py:82
  1251.6 8.9 reduce.11
  1266.0 6.9 copy.132
  1278.5 7.0 multiply_reduce_fusion.2
  1285.6 38.8 %psum.60 = f32[]{:T(128)} all-reduce(f32[]{:T(128)} %get-tuple-element.72), channel_id=1, replica_groups=mesh['px'=8,'py'=4] {'px','py'}, use_global_device_ids=true, to_apply=%region_9.10 | all-reduce | flops 1 | bytes 8 | tf_op jit(solution)/shard_map/psum | solution.py:135
  1346.5 40.3 %psum.61 = f32[]{:T(128)} all-reduce(f32[]{:T(128)} %get-tuple-element.8), channel_id=1, replica_groups=mesh['px'=8,'py'=4] {'px','py'}, use_global_device_ids=true, to_apply=%region_11.12 | all-reduce | flops 1 | bytes 8 | tf_op jit(solution)/shard_map/psum | solution.py:142
  1405.5 30.3 %all_to_all.335 = f32[4,1,131072]{2,1,0:T(1,128)} all-to-all(f32[4,1,131072]{2,1,0:T(1,128)} %reshape.119), channel_id=1, replica_groups=mesh['px'=8,'py'=4] {'py'}, dimensions={0} | all-to-all | bytes 4194304 | tf_op jit(solution)/shard_map/all_to_all | solution.py:65
  1435.8 8.9 reduce.12
  1450.2 6.9 copy.131
  1473.9 7.2 reshape.121
  1481.0 54.2 %all_to_all.336 = f32[8,1,65536]{2,1,0:T(1,128)} all-to-all(f32[8,1,65536]{2,1,0:T(1,128)} %reshape.121), channel_id=1, replica_groups=mesh['px'=8,'py'=4] {'px'}, dimensions={0} | all-to-all | bytes 4194304 | tf_op jit(solution)/shard_map/all_to_all | solution.py:68
  1535.3 8.4 reduce.13
  1575.6 7.2 reshape.123
  1582.8 52.0 %all_to_all.337 = f32[8,1,65536]{2,1,0:T(1,128)} all-to-all(f32[8,1,65536]{2,1,0:T(1,128)} %reshape.123), channel_id=1, replica_groups=mesh['px'=8,'py'=4] {'px'}, dimensions={0} | all-to-all | bytes 4194304 | tf_op jit(solution)/shard_map/all_to_all | solution.py:79
  1634.7 8.4 reduce.14
  1674.3 30.1 %all_to_all.338 = f32[4,1,131072]{2,1,0:T(1,128)} all-to-all(f32[4,1,131072]{2,1,0:T(1,128)} %reshape.125), channel_id=1, replica_groups=mesh['px'=8,'py'=4] {'py'}, dimensions={0} | all-to-all | bytes 4194304 | tf_op jit(solution)/shard_map/all_to_all | solution.py:82
  1704.4 8.9 reduce.15
  1718.8 6.9 copy.130
  1731.2 7.7 multiply_reduce_fusion
  1738.9 38.8 %psum.62 = f32[]{:T(128)} all-reduce(f32[]{:T(128)} %get-tuple-element.74), channel_id=1, replica_groups=mesh['px'=8,'py'=4] {'px','py'}, use_global_device_ids=true, to_apply=%region_13.14 | all-reduce | flops 1 | bytes 8 | tf_op jit(solution)/shard_map/psum | solution.py:135
  1798.9 40.3 %psum.63 = f32[]{:T(128)} all-reduce(f32[]{:T(128)} %fusion.6), channel_id=1, replica_groups=mesh['px'=8,'py'=4] {'px','py'}, use_global_device_ids=true, to_apply=%region_15.16 | all-reduce | flops 1 | bytes 8 | tf_op jit(solution)/shard_map/psum | solution.py:142
  1840.5 6.8 multiply_add_fusion.1
  1853.8 23.8 %all-to-all-done.17 = f32[32,64,256]{2,1,0:T(8,128)} async-done(((f32[32,64,256]{2,1,0:T(8,128)}), f32[32,64,256]{2,1,0:T(8,128)}, u32[]{:S(2)}, u32[]{:S(2)}) %all-to-all-start.17) | async-done | bytes 2097184 | tf_op jit(solution)/shard_map/all_to_all | solution.py:150
  (243 shorter events, 583.4 us)
Async XLA Ops:
  9.9 4.6 copy-start
  9.9 31.4 %all-to-all-start = ((f32[8,256,256]{2,0,1:T(8,128)}), f32[8,256,256]{2,0,1:T(8,128)}, u32[]{:S(2)}, u32[]{:S(2)}) async-start(f32[8,256,256]{2,0,1:T(8,128)} %get-tuple-element.19), calls=%async_computation | async-start | bytes 4194304 | tf_op jit(solution)/shard_map/all_to_all | solution.py:95
  14.5 10.2 collective-permute-start.2
  17.5 7.4 collective-permute-start
  25.0 1.4 copy-start.25
  26.4 27.9 %collective-permute-start.6 = (f32[34,1,256]{2,1,0:T(1,128)S(1)}, f32[34,1,256]{2,1,0:T(1,128)S(1)}, u32[]{:S(2)}, u32[]{:S(2)}) collective-permute-start(f32[34,1,256]{2,1,0:T(1,128)S(1)} %get-tuple-element.28), channel_id=1, source_target_pairs={{0,1},{1,2},{2,3},{3,0},{4,5},{5,6},{6,7},{7,4},{8,9},{9,10},{10,1... | collective-permute-start | bytes 104456 | tf_op jit(solution)/shard_map/ppermute | solution.py:32
  26.6 27.7 %collective-permute-start.4 = (f32[34,1,256]{2,1,0:T(1,128)S(1)}, f32[34,1,256]{2,1,0:T(1,128)S(1)}, u32[]{:S(2)}, u32[]{:S(2)}) collective-permute-start(f32[34,1,256]{2,1,0:T(1,128)S(1)} %get-tuple-element.29), channel_id=1, source_target_pairs={{1,0},{2,1},{3,2},{0,3},{5,4},{6,5},{7,6},{4,7},{9,8},{10,9},{11,1... | collective-permute-start | bytes 104456 | tf_op jit(solution)/shard_map/ppermute | solution.py:34
  43.5 11.9 copy-start.3
  43.6 8.2 collective-permute-start.3
  45.9 5.9 collective-permute-start.1
  51.8 2.5 collective-permute-start.5
  51.9 3.6 collective-permute-start.7
  69.9 1.3 copy-start.22
  162.7 53.6 %all-to-all-start.2 = ((f32[8,1,65536]{2,1,0:T(1,128)}), f32[8,1,65536]{2,1,0:T(1,128)}, u32[]{:S(2)}, u32[]{:S(2)}) async-start(f32[8,1,65536]{2,1,0:T(1,128)} %reshape.97), calls=%async_computation.2 | async-start | bytes 4194304 | tf_op jit(solution)/shard_map/all_to_all | solution.py:68
  418.4 7.5 collective-permute-start.9
  419.9 6.1 collective-permute-start.8
  423.2 6.3 copy-start.17
  423.2 6.3 copy-start.23
  426.0 3.6 copy-start.13
  426.0 1.9 collective-permute-start.10
  426.1 3.4 copy-start.5
  426.1 3.4 copy-start.9
  426.1 3.4 collective-permute-start.11
  481.7 1.3 copy-start.21
  873.8 11.6 copy-start.1
  873.8 7.1 collective-permute-start.13
  876.1 5.0 collective-permute-start.12
  878.6 6.8 copy-start.18
  881.1 4.3 copy-start.14
  881.1 1.7 collective-permute-start.14
  881.2 4.1 copy-start.6
  881.2 4.1 copy-start.10
  881.2 4.1 collective-permute-start.15
  936.0 1.3 copy-start.4
  1328.3 11.6 copy-start.2
  1328.3 7.1 collective-permute-start.17
  1330.7 5.0 collective-permute-start.16
  1333.1 6.8 copy-start.19
  1335.6 4.3 copy-start.15
  1335.7 1.7 collective-permute-start.18
  1335.8 4.2 copy-start.7
  1335.8 4.2 copy-start.11
  1335.8 4.1 collective-permute-start.19
  1781.6 7.1 collective-permute-start.21
  1784.0 5.0 collective-permute-start.20
  1786.4 6.8 copy-start.20
  1788.9 4.2 copy-start.16
  1789.0 1.7 collective-permute-start.22
  1789.1 4.1 copy-start.8
  1789.1 4.1 copy-start.12
  1789.1 4.1 collective-permute-start.23
  1847.3 4.6 copy-start.24
  1847.3 30.3 %all-to-all-start.17 = ((f32[32,64,256]{2,1,0:T(8,128)}), f32[32,64,256]{2,1,0:T(8,128)}, u32[]{:S(2)}, u32[]{:S(2)}) async-start(f32[32,64,256]{2,1,0:T(8,128)} %multiply_add_fusion.1), calls=%async_computation.17 | async-start | bytes 4194304 | tf_op jit(solution)/shard_map/all_to_all | solution.py:150
where the time goes:
time: 1890 us; the launch traced here: 1880 us
  blocking collectives  889 us (47%)
  local copies, waits for them, and re-layouts  485 us (26%)
  other arithmetic  225 us (12%)
  matrix products  118 us (6%)
  waiting for transfers between devices  102 us (5%)
  starting transfers between devices  50.2 us (3%)
    all_to_all x4, blocking collectives, precondition_cas(): lax.all_to_all(spectrum, 'px', split_axis=0, concat_axis=1, tiled=True)  209 us
    unnamed x87, local copies, waits for them, and re-layouts  194 us
    all_to_all x3, blocking collectives, precondition_cas(): lax.all_to_all(spectrum, 'px', split_axis=1, concat_axis=0, tiled=True)  163 us
    psum x4, blocking collectives, product_sum(): return lax.psum(jnp.sum(residual * precond), ('px', 'py'))  155 us
    all_to_all x4, blocking collectives, precondition_cas(): lax.all_to_all(spectrum, 'py', split_axis=2, concat_axis=1, tiled=True)  121 us
    psum x3, blocking collectives, local(): alpha = product_now / lax.psum(jnp.sum(direction * image), ('px', 'py'))  121 us
    all_to_all x4, blocking collectives, precondition_cas(): lax.all_to_all(spectrum, 'py', split_axis=1, concat_axis=2, tiled=True)  120 us
    unnamed x16, matrix products  71.8 us
  transfers between devices with their start and end apart: 27, of which 17 were waited for; matrix products, arithmetic and copies ran while one was open for 1% of the time, Pallas kernels for 0%

commit v1 on v0

v1 whole, which is shorter than its diff:
```python
import functools
import math

import jax
import jax.numpy as jnp
import numpy as np
from jax import lax
from jax.experimental import pallas as pl
from jax.experimental.pallas import tpu as pltpu
from jax.sharding import PartitionSpec as P

ITERS = 4
mass_rate = 0.01
mean_conduct = 1.0
excite_gain = 8.0
threshold = 0.15
base_rate = 0.002
rate_slope = 0.2
rate_shift = 0.3
time_step = 0.1
alpha_low = 0.199
alpha_high = 5.03

AXES = ("px", "py")
SUB = 8
LANE = 128
VMEM = pltpu.MemorySpace.VMEM


def cas_parts(length):
    steps = np.arange(length)
    angle = 2.0 * np.pi / length * (steps[:, None] * steps[None, :] % length)
    table = np.cos(angle) + np.sin(angle)
    high = table.astype(jnp.bfloat16)
    low = (table - high.astype(np.float64)).astype(jnp.bfloat16)
    return high, low


def wave_term(length):
    return 2.0 - 2.0 * np.cos(2.0 * np.pi / length * np.arange(length))


def mode_tables(gx, gy, gz, planes):
    sigma = mass_rate / mean_conduct + wave_term(gy)[:, None] + wave_term(gz)[None, :]
    rho = 1.0 / (1.0 + 0.5 * sigma + np.sqrt(sigma + 0.25 * sigma * sigma))
    scale = rho / (1.0 - rho * rho) / (mean_conduct * gy * gz)
    block = rho**planes
    closure = 1.0 / (1.0 - rho**gx)
    return rho, scale, block, closure


def split_bf16(x):
    high = x.astype(jnp.bfloat16)
    low = (x - high.astype(jnp.float32)).astype(jnp.bfloat16)
    return high, low


def dot(a, b):
    return jnp.dot(a, b, preferred_element_type=jnp.float32)


def right_transform(xh, xl, hh, hl):
    return dot(xh, hh) + dot(xl, hh) + dot(xh, hl)


def left_transform(xh, xl, hh, hl):
    return dot(hh, xh) + dot(hh, xl) + dot(hl, xh)


class Shape:
    def __init__(self, planes, gy, gz, devices):
        self.planes, self.gy, self.gz, self.devices = planes, gy, gz, devices
        self.gx = planes * devices
        self.halves = gz // LANE
        self.per_group = 2 * self.halves
        self.slots = gy // SUB * self.per_group // devices
        assert self.per_group % self.slots == 0
        self.rows = self.slots * SUB

    def place(self, group, kind, half):
        q = kind * self.halves + half
        return group * (self.per_group // self.slots) + q // self.slots, q % self.slots * SUB


def emit_forward(sh, source, rho, hh_ref, hl_ref, f_ref, pay_ref, scal):
    hh = hh_ref[...]
    hl = hl_ref[...]

    def plane(j, _):
        xh, xl = split_bf16(source(j))
        th, tl = split_bf16(right_transform(xh, xl, hh, hl))
        f_ref[j] = left_transform(th, tl, hh, hl)
        return 0

    lax.fori_loop(0, sh.planes, plane, 0)

    def group(g, _):
        row = pl.multiple_of(g * SUB, SUB)
        for half in range(sh.halves):
            lanes = slice(half * LANE, (half + 1) * LANE)
            decay = rho[pl.ds(row, SUB), lanes]
            f = [f_ref[j, pl.ds(row, SUB), lanes] for j in range(sh.planes)]
            p = f[0]
            e = f[-1]
            for j in range(1, sh.planes):
                p = f[j] + decay * p
                e = f[sh.planes - 1 - j] + decay * e
            for kind, value in ((0, p), (1, e)):
                d, at = sh.place(g, kind, half)
                pay_ref[d, pl.ds(at, SUB), :] = value
        return 0

    lax.fori_loop(0, sh.gy // SUB, group, 0)

    def spread(d, _):
        pay_ref[d, pl.ds(sh.rows, SUB), :] = scal
        return 0

    lax.fori_loop(0, sh.devices, spread, 0)


def stencil(sh, j, here, before, after, gx_ref, gy_ref, gz_ref):
    acc = gx_ref[j + 1] * (here - after) - gx_ref[j] * (before - here)
    flux = gy_ref[j] * (here - pltpu.roll(here, sh.gy - 1, 0))
    acc = acc + flux - pltpu.roll(flux, 1, 0)
    flux = gz_ref[j] * (here - pltpu.roll(here, sh.gz - 1, 1))
    return acc + flux - pltpu.roll(flux, 1, 1)


def fold(sh, x):
    return jnp.sum(x.reshape(sh.gy // SUB, SUB, sh.gz), axis=0)


def scal_tile(sh, parts):
    rows = []
    for part in parts:
        row = jnp.sum(part, axis=0, keepdims=True)
        total = row[:, :LANE]
        for half in range(1, sh.halves):
            total = total + row[:, half * LANE : (half + 1) * LANE]
        rows.append(total)
    rows.append(jnp.zeros((SUB - len(rows), LANE), jnp.float32))
    return jnp.concatenate(rows, axis=0)


def start_kernel(
    sh, parts, u, ulo, uhi, craw, clo, chi, rho, hh, hl, gx, gy, gz, r, f, pay, c
):
    wide = sh.gy // parts
    for k in range(parts):
        c[:, k * wide : (k + 1) * wide, :] = 0.5 * craw[k]

    def faces(j, _):
        own = c[j]
        gy[j] = own + pltpu.roll(own, sh.gy - 1, 0)
        gz[j] = own + pltpu.roll(own, sh.gz - 1, 1)
        return 0

    lax.fori_loop(0, sh.planes, faces, 0)
    gx[0] = 0.5 * clo[0] + c[0]
    gx[sh.planes] = 0.5 * chi[0] + c[sh.planes - 1]

    def cross(j, _):
        gx[j] = c[j - 1] + c[j]
        return 0

    lax.fori_loop(1, sh.planes, cross, 0)

    last = sh.planes - 1
    r[0] = -stencil(sh, 0, u[0], ulo[0], u[1], gx, gy, gz)

    def inner(j, _):
        r[j] = -stencil(sh, j, u[j], u[j - 1], u[j + 1], gx, gy, gz)
        return 0

    lax.fori_loop(1, last, inner, 0)
    r[last] = -stencil(sh, last, u[last], u[last - 1], uhi[0], gx, gy, gz)
    emit_forward(
        sh, lambda j: r[j], rho, hh, hl, f, pay, jnp.zeros((SUB, LANE), jnp.float32)
    )


def scan_kernel(sh, first, *refs):
    recv, decay, closure, onward = refs[:4]
    if first:
        (out,) = refs[4:]
    else:
        coef, out, coef_out = refs[4:]
    count = sh.devices

    def run(rows, forward, store):
        a = decay[rows]
        order = (lambda i: i) if forward else (lambda i: count - 1 - i)

        def total(i, s):
            return recv[order(i), rows, :] + a * s

        zero = jnp.zeros(a.shape, jnp.float32)
        carry = lax.fori_loop(0, count, total, zero, unroll=8) * closure[rows]

        def step(i, carry):
            store(order(i), carry)
            return recv[order(i), rows, :] + a * carry

        lax.fori_loop(0, count, step, carry, unroll=8)

    if sh.slots == sh.per_group:
        half = sh.rows // 2
        for rows, forward in ((slice(0, half), True), (slice(half, sh.rows), False)):

            def store(d, x, rows=rows):
                out[d, rows, :] = x

            run(rows, forward, store)
    else:
        rows = slice(0, sh.rows)
        take = onward[...]

        def store_forward(d, x):
            out[d] = x

        def store_backward(d, x):
            out[d] = jnp.where(take > 0.5, out[d], x)

        run(rows, True, store_forward)
        run(rows, False, store_backward)

    if not first:
        sums = sum_rows(sh.devices, recv, sh.rows)
        coef_out[...] = next_coefficients(sums, coef[...], sh.gz)


def sum_rows(count, recv, at):
    def add(d, s):
        return s + recv[d, at : at + SUB, :]

    return lax.fori_loop(1, count, add, recv[0, at : at + SUB, :], unroll=4)


def next_coefficients(sums, previous, width):
    product = jnp.maximum(jnp.sum(sums[0:1], axis=1, keepdims=True), 0.0)
    curve = jnp.sum(sums[1:2], axis=1, keepdims=True)
    product = jnp.broadcast_to(product, (1, width))
    curve = jnp.broadcast_to(curve, (1, width))
    old_product = previous[0:1]
    old_alpha = previous[1:2]
    started = old_product > 0.0
    beta = jnp.where(started, product / jnp.where(started, old_product, 1.0), 0.0)
    curve = curve - beta * product / jnp.where(old_alpha > 0.0, old_alpha, 1.0)
    usable = curve > 0.0
    alpha = jnp.where(usable, product / jnp.where(usable, curve, 1.0), alpha_low)
    alpha = jnp.clip(alpha, alpha_low, alpha_high)
    return jnp.concatenate(
        [product, alpha, beta, jnp.zeros((SUB - 3, width), jnp.float32)], axis=0
    )


def emit_inverse(sh, f, carry, rho, scale, hh_ref, hl_ref, uh, ul, m):
    tall = 2 * SUB

    def group(i, _):
        row = pl.multiple_of(i * tall, tall)
        for half in range(sh.halves):
            lanes = slice(half * LANE, (half + 1) * LANE)
            decay = rho[pl.ds(row, tall), lanes]
            gain = scale[pl.ds(row, tall), lanes]
            ends = []
            for kind in range(2):
                tiles = []
                for g in (2 * i, 2 * i + 1):
                    d, at = sh.place(g, kind, half)
                    tiles.append(carry[d, pl.ds(at, SUB), :])
                ends.append(jnp.concatenate(tiles, axis=0))
            first, final = ends

            def put(j, value):
                high, low = split_bf16(gain * value)
                uh[j, pl.ds(row, tall), lanes] = high
                ul[j, pl.ds(row, tall), lanes] = low

            fields = [f[j, pl.ds(row, tall), lanes] for j in range(sh.planes)]
            back = [None] * sh.planes
            e = final
            for j in reversed(range(sh.planes)):
                back[j] = decay * e
                e = fields[j] + back[j]
            put(0, first + decay * e)
            p = first
            for j in range(sh.planes):
                p = fields[j] + decay * p
                put(j + 1, p + back[j])
            put(sh.planes + 1, decay * p + final)
        return 0

    lax.fori_loop(0, sh.gy // tall, group, 0)
    hh = hh_ref[...]
    hl = hl_ref[...]

    def plane(j, _):
        th, tl = split_bf16(right_transform(uh[j], ul[j], hh, hl))
        m[j] = left_transform(th, tl, hh, hl)
        return 0

    lax.fori_loop(0, sh.planes + 2, plane, 0)


def step_kernel(sh, stage, *refs):
    names = ["f", "carry", "rho", "scale", "hh", "hl", "gx", "gy", "gz", "r"]
    if stage > 0:
        names += ["coef", "z", "w"]
    if stage > 1:
        names += ["s", "q", "t"]
    last = stage == ITERS - 1
    if stage == 0:
        outs = ["z_new", "w_new"]
    elif last:
        outs = ["z_new"]
    else:
        outs = ["z_new", "w_new", "r_new", "s_new", "q_new", "t_new"]
        if stage == 1:
            outs.remove("s_new")
    outs += ["pay"] if last else ["f_new", "pay"]
    scratch = ["uh", "ul", "m"]
    if last:
        scratch += []
    k = dict(zip(names + outs + scratch, refs, strict=True))
    m = k["m"]
    emit_inverse(sh, k["f"], k["carry"], k["rho"], k["scale"], k["hh"], k["hl"], k["uh"], k["ul"], m)
    if stage > 0:
        alpha = k["coef"][1:2, :]
        beta = k["coef"][2:3, :]

    def plane(j, sums):
        here = m[j + 1]
        image = mass_rate * here + mean_conduct * stencil(
            sh, j, here, m[j], m[j + 2], k["gx"], k["gy"], k["gz"]
        )
        if stage == 0:
            z, w, r = here, image, k["r"][j]
        else:
            s, q, t = k["w"][j], here, image
            if stage > 1:
                s = s + beta * k["s"][j]
                q = q + beta * k["q"][j]
                t = t + beta * k["t"][j]
            r = k["r"][j] - alpha * s
            z = k["z"][j] - alpha * q
            w = k["w"][j] - alpha * t
            if not last:
                k["r_new"][j] = r
                k["q_new"][j] = q
                k["t_new"][j] = t
                if stage > 1:
                    k["s_new"][j] = s
        k["z_new"][j] = z
        if not last:
            k["w_new"][j] = w
        return (sums[0] + fold(sh, r * z), sums[1] + fold(sh, w * z))

    zero = jnp.zeros((SUB, sh.gz), jnp.float32)
    scal = scal_tile(sh, lax.fori_loop(0, sh.planes, plane, (zero, zero)))
    if last:
        pay = k["pay"]

        def spread(d, _):
            pay[d] = scal
            return 0

        lax.fori_loop(0, sh.devices, spread, 0)
    else:
        w_new = k["w_new"]
        emit_forward(sh, lambda j: w_new[j], k["rho"], k["hh"], k["hl"], k["f_new"], k["pay"], scal)


def finish_kernel(sh, *refs):
    coefs = refs[: ITERS - 1]
    recv = refs[ITERS - 1]
    u = refs[ITERS]
    fields = refs[ITERS + 1 : 2 * ITERS + 1]
    out = refs[-1]
    rows = [c[...] for c in coefs]
    rows.append(next_coefficients(sum_rows(sh.devices, recv, 0), rows[-1], sh.gz))
    weight = rows[-1][1:2]
    weights = [weight]
    for i in reversed(range(ITERS - 1)):
        weight = rows[i][1:2] + rows[i + 1][2:3] * weight
        weights.insert(0, weight)

    def plane(j, _):
        total = u[j]
        for weight, field in zip(weights, fields):
            total = total + weight * field[j]
        out[j] = total
        return 0

    lax.fori_loop(0, sh.planes, plane, 0)


def call(kernel, name, out_shapes, operands, scratch=(), aliases=None):
    whole = pl.BlockSpec(memory_space=VMEM)
    return pl.pallas_call(
        kernel,
        name=name,
        out_shape=[jax.ShapeDtypeStruct(s, jnp.float32) for s in out_shapes],
        in_specs=[whole] * len(operands),
        out_specs=[whole] * len(out_shapes),
        scratch_shapes=list(scratch),
        input_output_aliases=aliases or {},
        compiler_params=pltpu.CompilerParams(vmem_limit_bytes=60 * 1024 * 1024),
    )(*operands)


def exchange(x):
    return lax.all_to_all(x, AXES, split_axis=0, concat_axis=0, tiled=True)


def neighbours(first, final, axes):
    count = lax.axis_size(axes)
    return (
        lax.ppermute(final, axes, [(i, (i + 1) % count) for i in range(count)]),
        lax.ppermute(first, axes, [((i + 1) % count, i) for i in range(count)]),
    )


def local(potential, recovery, stimulus, conductivity):
    parts = lax.axis_size("py")
    devices = lax.axis_size("px") * parts
    planes, gy, gz = potential.shape
    sh = Shape(planes, gy, gz, devices)

    wide = conductivity.shape[1]
    craw = lax.all_to_all(
        conductivity.reshape(parts, planes, wide, gz), "py", split_axis=0, concat_axis=0, tiled=True
    )
    drive = (
        excite_gain * potential * (potential - threshold) * (1.0 - potential) - potential * recovery
    )
    v_star = potential + time_step * (drive + stimulus)
    rate = base_rate + rate_slope * recovery / (potential + rate_shift)
    recovery_next = recovery + time_step * rate * (
        -recovery - excite_gain * potential * (potential - threshold - 1.0)
    )
    ulo, uhi = neighbours(v_star[:1], v_star[-1:], AXES)

    def edge(j):
        return craw[:, j].reshape(1, gy, gz)

    clo, chi = neighbours(edge(0), edge(planes - 1), AXES)

    rho, scale, block, closure = mode_tables(sh.gx, gy, gz, planes)
    groups = gy // SUB

    def own_tiles(table):
        tiles = table.astype(np.float32).reshape(groups, SUB, sh.halves, LANE).transpose(0, 2, 1, 3)
        both = np.concatenate([tiles, tiles], axis=1).reshape(devices, sh.rows, LANE)
        return lax.dynamic_index_in_dim(jnp.asarray(both), lax.axis_index(AXES), 0, False)

    block = own_tiles(block)
    closure = own_tiles(closure)
    slot = lax.axis_index(AXES) * sh.slots + jnp.arange(sh.rows, dtype=jnp.int32)[:, None] // SUB
    onward = jnp.broadcast_to(
        (slot % sh.per_group < sh.halves).astype(jnp.float32), (sh.rows, LANE)
    )
    rho = jnp.asarray(rho.astype(np.float32))
    scale = jnp.asarray(scale.astype(np.float32))
    hh, hl = (jnp.asarray(x) for x in cas_parts(gy))

    slab = (planes, gy, gz)
    payload = (devices, sh.rows + SUB, LANE)
    carries = (devices, sh.rows, LANE)
    tables = [rho, hh, hl]
    gxf, gyf, gzf, r, f, pay = call(
        functools.partial(start_kernel, sh, parts),
        "start",
        [(planes + 1, gy, gz), slab, slab, slab, slab, payload],
        [v_star, ulo, uhi, craw, clo, chi] + tables,
        [pltpu.VMEM(slab, jnp.float32)],
    )
    spectral = [
        pltpu.VMEM((planes + 2, gy, gz), jnp.bfloat16),
        pltpu.VMEM((planes + 2, gy, gz), jnp.bfloat16),
        pltpu.VMEM((planes + 2, gy, gz), jnp.float32),
    ]
    coef = jnp.zeros((SUB, gz), jnp.float32)
    coefs = []
    basis = []
    z = w = s = q = t = None
    for stage in range(ITERS):
        recv = exchange(pay)
        if stage == 0:
            (carry,) = call(
                functools.partial(scan_kernel, sh, True),
                "scan0",
                [carries],
                [recv, block, closure, onward],
            )
        else:
            carry, coef = call(
                functools.partial(scan_kernel, sh, False),
                f"scan{stage}",
                [carries, (SUB, gz)],
                [recv, block, closure, onward, coef],
            )
            coefs.append(coef)
        carry = exchange(carry)
        operands = [f, carry, rho, scale, hh, hl, gxf, gyf, gzf, r]
        if stage > 0:
            operands += [coef, z, w]
        if stage > 1:
            operands += [s, q, t]
        kernel = functools.partial(step_kernel, sh, stage)
        if stage == 0:
            z, w, f, pay = call(kernel, "step0", [slab, slab, slab, payload], operands, spectral)
        elif stage < ITERS - 1:
            shapes = [slab] * (5 if stage == 1 else 6) + [slab, payload]
            old_w = w
            results = call(kernel, f"step{stage}", shapes, operands, spectral)
            if stage == 1:
                z, w, r, q, t, f, pay = results
                s = old_w
            else:
                z, w, r, s, q, t, f, pay = results
        else:
            z, pay = call(kernel, f"step{stage}", [slab, (devices, SUB, LANE)], operands, spectral)
        basis.append(z)
    recv = exchange(pay)
    (potential_next,) = call(
        functools.partial(finish_kernel, sh), "finish", [slab], coefs + [recv, v_star] + basis
    )
    return potential_next, recovery_next


def solution(mesh):
    in_specs = (
        P(AXES, None, None),
        P(AXES, None, None),
        P(AXES, None, None),
        P("px", "py", None),
    )
    out_specs = (P(AXES, None, None), P(AXES, None, None))
    return jax.shard_map(local, mesh=mesh, in_specs=in_specs, out_specs=out_specs, check_vma=False)
```

time: 1890 us -> 358 us (0.19)
  blocking collectives: 889 us -> 152 us
  local copies, waits for them, and re-layouts: 485 us -> 5.8 us
  other arithmetic: 225 us -> 4.55 us
  Pallas kernels: 0 us -> 134 us
  matrix products: 118 us -> 0 us
  waiting for transfers between devices: 102 us -> 38.2 us
  starting transfers between devices: 50.2 us -> 22 us
    all_to_all x15 -> x8, blocking collectives: 613 us -> 152 us  [exchange(): return lax.all_to_all(x, AXES, split_axis=0, concat_axis=0, tiled=True)]
    psum x7 -> x0, blocking collectives: 276 us -> none  [the longest x4 155 us: product_sum(): return lax.psum(jnp.sum(residual * precond), ('px', 'py'))]
    unnamed x87 -> x12, local copies, waits for them, and re-layouts: 194 us -> 1.4 us
    all_to_all x35 -> x0, local copies, waits for them, and re-layouts: 186 us -> none  [the longest x9 50.3 us: precondition_cas(): lax.all_to_all(spectrum, 'py', split_axis=2, concat_axis=1, tiled=True)]
    all_to_all x16 -> x0, other arithmetic: 139 us -> none  [the longest x4 35.8 us: precondition_cas(): lax.all_to_all(spectrum, 'py', split_axis=1, concat_axis=2, tiled=True)]
    pallas_call x0 -> x10, Pallas kernels: none -> 134 us  [call(): pl.pallas_call(kernel, name=name, out_shape=[jax.ShapeDtypeStruct(s, jnp....]
    unnamed x16 -> x0, matrix products: 71.8 us -> none
    all_to_all x3 -> x2, waiting for transfers between devices: 84.5 us -> 34.1 us  [the longest x1 17.5 us: local(): lax.all_to_all(conductivity.reshape(parts, planes, wide, gz), 'py', split...]
  transfers between devices with their start and end apart: 27 -> 6, of which waited for: 17 -> 3; matrix products, arithmetic and copies ran while one was open for 1% -> 2% of each run, Pallas kernels for 0% -> 0%
where the time goes in v1:
time: 358 us; the launch traced here: 357 us
  blocking collectives  152 us (42%)
  Pallas kernels  134 us (37%)
  waiting for transfers between devices  38.2 us (11%)
  starting transfers between devices  22 us (6%)
  local copies, waits for them, and re-layouts  5.8 us (2%)
  other arithmetic  4.55 us (1%)
    all_to_all x8, blocking collectives, exchange(): return lax.all_to_all(x, AXES, split_axis=0, concat_axis=0, tiled=True)  152 us
    pallas_call x10, Pallas kernels, call(): pl.pallas_call(kernel, name=name, out_shape=[jax.ShapeDtypeStruct(s, jnp....  134 us
    all_to_all x1, waiting for transfers between devices, local(): lax.all_to_all(conductivity.reshape(parts, planes, wide, gz), 'py', split...  17.5 us
    all_to_all x1, waiting for transfers between devices, exchange(): return lax.all_to_all(x, AXES, split_axis=0, concat_axis=0, tiled=True)  16.6 us
    ppermute x2, starting transfers between devices, neighbours(): lax.ppermute(first, axes, [((i + 1) % count, i) for i in range(count)])  12.5 us
  transfers between devices with their start and end apart: 6, of which 3 were waited for; matrix products, arithmetic and copies ran while one was open for 2% of the time, Pallas kernels for 0%

profile of v1, /device:TPU:0, one launch (start us, length us, event | category | flops | bytes accessed | tf_op | source)
XLA Modules:
  0.0 357.0 jit_solution(13379773082913568913)
XLA Ops:
  0.6 4.5 %all-to-all-start = ((f32[4,8,64,256]{3,2,1,0:T(8,128)}), f32[4,8,64,256]{3,2,1,0:T(8,128)}, u32[]{:S(2)}, u32[]{:S(2)}) async-start(f32[4,8,64,256]{3,2,1,0:T(8,128)} %bitcast.5), calls=%async_computation | async-start | bytes 4194304 | tf_op jit(solution)/shard_map/all_to_all | solution.py:432
  5.1 4.5 %multiply_add_fusion = (f32[8,256,256]{2,1,0:T(8,128)}, f32[8,256,256]{2,1,0:T(8,128)S(1)}) fusion(f32[8,256,256]{2,1,0:T(8,128)} %param.11, f32[8,256,256]{2,1,0:T(8,128)} %param.10, f32[8,256,256]{2,1,0:T(8,128)} %param.12), kind=kLoop, calls=%fused_computation | loop fusion | flops 11010048 | bytes 10485760 | tf_op jit(solution)/shard_map/add | solution.py:440
  9.6 0.0 copy-start
  9.7 7.2 %collective-permute-start.1 = (f32[1,256,256]{2,1,0:T(8,128)S(1)}, f32[1,256,256]{2,1,0:T(8,128)S(1)}, u32[]{:S(2)}, u32[]{:S(2)}) collective-permute-start(f32[1,256,256]{2,1,0:T(8,128)S(1)} %get-tuple-element.72), channel_id=1, source_target_pairs={{1,0},{2,1},{3,2},{4,3},{5,4},{6,5},{7,6},{8,7},{9,8},{10,9},{11,1... | collective-permute-start | bytes 786440 | tf_op jit(solution)/shard_map/ppermute | solution.py:421
  16.9 0.0 collective-permute-start
  16.9 17.5 %all-to-all-done.craw = f32[4,8,64,256]{3,2,1,0:T(8,128)} async-done(((f32[4,8,64,256]{3,2,1,0:T(8,128)}), f32[4,8,64,256]{3,2,1,0:T(8,128)}, u32[]{:S(2)}, u32[]{:S(2)}) %all-to-all-start) | async-done | bytes 2097184 | tf_op jit(solution)/shard_map/all_to_all | solution.py:432
  34.4 1.1 fusion.2
  35.4 0.1 collective-permute-start.2
  35.5 5.3 %collective-permute-start.3 = (f32[1,256,256]{2,1,0:T(8,128)S(1)}, f32[1,256,256]{2,1,0:T(8,128)S(1)}, u32[]{:S(2)}, u32[]{:S(2)}) collective-permute-start(f32[1,256,256]{2,1,0:T(8,128)S(1)} %bitcast.6), channel_id=1, source_target_pairs={{1,0},{2,1},{3,2},{4,3},{5,4},{6,5},{7,6},{8,7},{9,8},{10,9},{11,1... | collective-permute-start | bytes 786440 | tf_op jit(solution)/shard_map/ppermute | solution.py:421
  40.8 0.0 collective-permute-done.1.uhi
  40.8 0.0 copy-start.2
  40.8 0.0 collective-permute-done.ulo
  40.8 0.0 copy-start.3
  40.8 4.0 %collective-permute-done.2.clo = f32[1,256,256]{2,1,0:T(8,128)S(1)} collective-permute-done((f32[1,256,256]{2,1,0:T(8,128)S(1)}, f32[1,256,256]{2,1,0:T(8,128)S(1)}, u32[]{:S(2)}, u32[]{:S(2)}) %collective-permute-start.2) | collective-permute-done | bytes 262176 | tf_op jit(solution)/shard_map/ppermute | solution.py:420
  44.9 0.0 copy-start.4
  44.9 0.0 collective-permute-done.3.chi
  44.9 0.0 copy-done
  44.9 0.0 copy-done.2
  44.9 0.0 copy-done.3
  44.9 0.7 copy-done.4
  45.6 0.0 copy-start.5
  45.6 0.7 copy-done.5
  46.3 16.6 %start.1 = (f32[9,256,256]{2,1,0:T(8,128)}, f32[8,256,256]{2,1,0:T(8,128)}, f32[8,256,256]{2,1,0:T(8,128)}, f32[8,256,256]{2,1,0:T(8,128)}, f32[8,256,256]{2,1,0:T(8,128)}, /*index=5*/f32[32,40,128]{2,1,0:T(8,128)}) custom-call(f32[8,256,256]{2,1,0:T(8,128)} %copy-done, f32[1,256,256]{2,1,0:T(8,128)} %copy-done.3, f32[1,256,256]{2,1,0:T(8,128)} %copy-done.2, ...), custom_call_target="tpu_custom_call" | custom-call | tf_op jit(solution)/shard_map/start/pallas_call | solution.py:401
  62.9 5.0 %all-to-all-start.1 = ((f32[32,40,128]{2,1,0:T(8,128)}), f32[32,40,128]{2,1,0:T(8,128)S(1)}, u32[]{:S(2)}, u32[]{:S(2)}) async-start(f32[32,40,128]{2,1,0:T(8,128)} %get-tuple-element.36), calls=%async_computation.1 | async-start | bytes 1310720 | tf_op jit(solution)/shard_map/all_to_all | solution.py:414
  67.9 1.3 dynamic-slice_bitcast_fusion.refs_1_
  69.3 16.6 %all-to-all-done.1.refs_0_ = f32[32,40,128]{2,1,0:T(8,128)S(1)} async-done(((f32[32,40,128]{2,1,0:T(8,128)}), f32[32,40,128]{2,1,0:T(8,128)S(1)}, u32[]{:S(2)}, u32[]{:S(2)}) %all-to-all-start.1) | async-done | bytes 655392 | tf_op jit(solution)/shard_map/all_to_all | solution.py:414
  85.9 0.0 copy-start.1
  85.9 0.8 broadcast_in_dim.4.refs_3_
  86.7 0.6 broadcast.93.refs_2_
  87.3 0.0 copy-done.1
  87.3 2.2 scan0.1
  89.5 19.1 %all_to_all.50.refs_1_ = f32[32,32,128]{2,1,0:T(8,128)} all-to-all(f32[32,32,128]{2,1,0:T(8,128)} %scan0.1), channel_id=1, replica_groups=mesh['px'=8,'py'=4] {'px','py'}, dimensions={0} | all-to-all | bytes 1048576 | tf_op jit(solution)/shard_map/all_to_all | solution.py:414
  108.6 23.7 %step0.1 = (f32[8,256,256]{2,1,0:T(8,128)}, f32[8,256,256]{2,1,0:T(8,128)}, f32[8,256,256]{2,1,0:T(8,128)}, f32[32,40,128]{2,1,0:T(8,128)}) custom-call(f32[8,256,256]{2,1,0:T(8,128)} %get-tuple-element.35.refs_0_, f32[32,32,128]{2,1,0:T(8,128)} %all_to_all.50.refs_1_, f32[256,256]{1,0:T(8,128)} %constant.83.clone.rho.refs_2_, ...), custom_call_target="tpu_custom_call" | custom-call | tf_op jit(solution)/shard_map/step0/pallas_call | solution.py:401
  132.3 21.3 %all_to_all.51.refs_0_ = f32[32,40,128]{2,1,0:T(8,128)} all-to-all(f32[32,40,128]{2,1,0:T(8,128)} %get-tuple-element.41), channel_id=1, replica_groups=mesh['px'=8,'py'=4] {'px','py'}, dimensions={0} | all-to-all | bytes 1310720 | tf_op jit(solution)/shard_map/all_to_all | solution.py:414
  153.6 0.6 broadcast_in_dim.10.refs_4_
  154.2 2.3 scan1.1
  156.5 19.0 %all_to_all.52.refs_1_ = f32[32,32,128]{2,1,0:T(8,128)} all-to-all(f32[32,32,128]{2,1,0:T(8,128)} %get-tuple-element.44), channel_id=1, replica_groups=mesh['px'=8,'py'=4] {'px','py'}, dimensions={0} | all-to-all | bytes 1048576 | tf_op jit(solution)/shard_map/all_to_all | solution.py:414
  175.5 27.5 %step1.1 = (f32[8,256,256]{2,1,0:T(8,128)}, f32[8,256,256]{2,1,0:T(8,128)}, f32[8,256,256]{2,1,0:T(8,128)}, f32[8,256,256]{2,1,0:T(8,128)}, f32[8,256,256]{2,1,0...) custom-call(f32[8,256,256]{2,1,0:T(8,128)} %get-tuple-element.43.refs_0_, f32[32,32,128]{2,1,0:T(8,128)} %all_to_all.52.refs_1_, ...), custom_call_target="tpu_custom_call" | custom-call | tf_op jit(solution)/shard_map/step1/pallas_call | solution.py:401
  203.1 21.3 %all_to_all.53.refs_0_ = f32[32,40,128]{2,1,0:T(8,128)} all-to-all(f32[32,40,128]{2,1,0:T(8,128)} %get-tuple-element.47), channel_id=1, replica_groups=mesh['px'=8,'py'=4] {'px','py'}, dimensions={0} | all-to-all | bytes 1310720 | tf_op jit(solution)/shard_map/all_to_all | solution.py:414
  224.4 2.3 scan2.1
  226.7 19.0 %all_to_all.54.refs_1_ = f32[32,32,128]{2,1,0:T(8,128)} all-to-all(f32[32,32,128]{2,1,0:T(8,128)} %get-tuple-element.50), channel_id=1, replica_groups=mesh['px'=8,'py'=4] {'px','py'}, dimensions={0} | all-to-all | bytes 1048576 | tf_op jit(solution)/shard_map/all_to_all | solution.py:414
  245.7 30.6 %step2.1 = (f32[8,256,256]{2,1,0:T(8,128)}, f32[8,256,256]{2,1,0:T(8,128)}, f32[8,256,256]{2,1,0:T(8,128)}, f32[8,256,256]{2,1,0:T(8,128)}, f32[8,256,256]{2,1,0...) custom-call(f32[8,256,256]{2,1,0:T(8,128)} %get-tuple-element.49.refs_0_, ...), custom_call_target="tpu_custom_call" | custom-call | tf_op jit(solution)/shard_map/step2/pallas_call | solution.py:401
  276.3 21.3 %all_to_all.55.refs_0_ = f32[32,40,128]{2,1,0:T(8,128)} all-to-all(f32[32,40,128]{2,1,0:T(8,128)} %get-tuple-element.56), channel_id=1, replica_groups=mesh['px'=8,'py'=4] {'px','py'}, dimensions={0} | all-to-all | bytes 1310720 | tf_op jit(solution)/shard_map/all_to_all | solution.py:414
  297.6 2.3 scan3.1
  299.8 19.0 %all_to_all.56.refs_1_ = f32[32,32,128]{2,1,0:T(8,128)} all-to-all(f32[32,32,128]{2,1,0:T(8,128)} %get-tuple-element.59), channel_id=1, replica_groups=mesh['px'=8,'py'=4] {'px','py'}, dimensions={0} | all-to-all | bytes 1048576 | tf_op jit(solution)/shard_map/all_to_all | solution.py:414
  318.9 20.4 %step3.1 = (f32[8,256,256]{2,1,0:T(8,128)}, f32[32,8,128]{2,1,0:T(8,128)}) custom-call(f32[8,256,256]{2,1,0:T(8,128)} %get-tuple-element.58.refs_0_, f32[32,32,128]{2,1,0:T(8,128)} %all_to_all.56.refs_1_, f32[256,256]{1,0:T(8,128)} %constant.83.clone.rho.refs_2_, f32[256,256]{1,0:T(8,128)} %constant.84.clone.refs_3_, ...), custom_call_target="tpu_custom_call" | custom-call | tf_op jit(solution)/shard_map/step3/pallas_call | solution.py:401
  339.3 11.5 %all_to_all.57.refs_3_ = f32[32,8,128]{2,1,0:T(8,128)} all-to-all(f32[32,8,128]{2,1,0:T(8,128)} %get-tuple-element.66), channel_id=1, replica_groups=mesh['px'=8,'py'=4] {'px','py'}, dimensions={0} | all-to-all | bytes 262144 | tf_op jit(solution)/shard_map/all_to_all | solution.py:414
  350.7 6.2 %finish.1 = f32[8,256,256]{2,1,0:T(8,128)} custom-call(f32[8,256]{1,0:T(8,128)} %get-tuple-element.42.refs_10_.refs_4_.refs_0_, f32[8,256]{1,0:T(8,128)} %get-tuple-element.48.refs_10_.refs_4_.refs_1_, f32[8,256]{1,0:T(8,128)} %get-tuple-element.57.refs_10_.refs_2_, f32[32,8,128]{2,1,0:T(8,128)} %all_to_all.57.refs_3_, f32[8,256,256]{2,1,0:T(8,128)} %copy-done, ...), custom_call_target="tpu_custom_call" | custom-call | tf_op jit(solution)/shard_map/finish/pallas_call | solution.py:401
  (2 shorter events, 0.0 us)
Async XLA Ops:
  0.6 33.7 %all-to-all-start = ((f32[4,8,64,256]{3,2,1,0:T(8,128)}), f32[4,8,64,256]{3,2,1,0:T(8,128)}, u32[]{:S(2)}, u32[]{:S(2)}) async-start(f32[4,8,64,256]{3,2,1,0:T(8,128)} %bitcast.5), calls=%async_computation | async-start | bytes 4194304 | tf_op jit(solution)/shard_map/all_to_all | solution.py:432
  9.6 35.2 %copy-start = (f32[8,256,256]{2,1,0:T(8,128)}, f32[8,256,256]{2,1,0:T(8,128)S(1)}, u32[]{:S(2)}) copy-start(f32[8,256,256]{2,1,0:T(8,128)S(1)} %get-tuple-element.69.u.refs_4_) | copy-start | bytes 6291460
  9.7 31.1 %collective-permute-start.1 = (f32[1,256,256]{2,1,0:T(8,128)S(1)}, f32[1,256,256]{2,1,0:T(8,128)S(1)}, u32[]{:S(2)}, u32[]{:S(2)}) collective-permute-start(f32[1,256,256]{2,1,0:T(8,128)S(1)} %get-tuple-element.72), channel_id=1, source_target_pairs={{1,0},{2,1},{3,2},{4,3},{5,4},{6,5},{7,6},{8,7},{9,8},{10,9},{11,1... | collective-permute-start | bytes 786440 | tf_op jit(solution)/shard_map/ppermute | solution.py:421
  16.9 24.0 %collective-permute-start = (f32[1,256,256]{2,1,0:T(8,128)S(1)}, f32[1,256,256]{2,1,0:T(8,128)S(1)}, u32[]{:S(2)}, u32[]{:S(2)}) collective-permute-start(f32[1,256,256]{2,1,0:T(8,128)S(1)} %get-tuple-element.73), channel_id=1, source_target_pairs={{0,1},{1,2},{2,3},{3,4},{4,5},{5,6},{6,7},{7,8},{8,9},{9,10},{10,1... | collective-permute-start | bytes 786440 | tf_op jit(solution)/shard_map/ppermute | solution.py:420
  35.4 9.4 %collective-permute-start.2 = (f32[1,256,256]{2,1,0:T(8,128)S(1)}, f32[1,256,256]{2,1,0:T(8,128)S(1)}, u32[]{:S(2)}, u32[]{:S(2)}) collective-permute-start(f32[1,256,256]{2,1,0:T(8,128)S(1)} %bitcast.7), channel_id=1, source_target_pairs={{0,1},{1,2},{2,3},{3,4},{4,5},{5,6},{6,7},{7,8},{8,9},{9,10},{10,1... | collective-permute-start | bytes 786440 | tf_op jit(solution)/shard_map/ppermute | solution.py:420
  35.5 9.4 %collective-permute-start.3 = (f32[1,256,256]{2,1,0:T(8,128)S(1)}, f32[1,256,256]{2,1,0:T(8,128)S(1)}, u32[]{:S(2)}, u32[]{:S(2)}) collective-permute-start(f32[1,256,256]{2,1,0:T(8,128)S(1)} %bitcast.6), channel_id=1, source_target_pairs={{1,0},{2,1},{3,2},{4,3},{5,4},{6,5},{7,6},{8,7},{9,8},{10,9},{11,1... | collective-permute-start | bytes 786440 | tf_op jit(solution)/shard_map/ppermute | solution.py:421
  40.8 4.1 %copy-start.2 = (f32[1,256,256]{2,1,0:T(8,128)}, f32[1,256,256]{2,1,0:T(8,128)S(1)}, u32[]{:S(2)}) copy-start(f32[1,256,256]{2,1,0:T(8,128)S(1)} %collective-permute-done.1.uhi) | copy-start | bytes 786436
  40.8 4.1 %copy-start.3 = (f32[1,256,256]{2,1,0:T(8,128)}, f32[1,256,256]{2,1,0:T(8,128)S(1)}, u32[]{:S(2)}) copy-start(f32[1,256,256]{2,1,0:T(8,128)S(1)} %collective-permute-done.ulo) | copy-start | bytes 786436
  44.9 0.7 copy-start.4
  45.6 0.7 copy-start.5
  62.9 23.0 %all-to-all-start.1 = ((f32[32,40,128]{2,1,0:T(8,128)}), f32[32,40,128]{2,1,0:T(8,128)S(1)}, u32[]{:S(2)}, u32[]{:S(2)}) async-start(f32[32,40,128]{2,1,0:T(8,128)} %get-tuple-element.36), calls=%async_computation.1 | async-start | bytes 1310720 | tf_op jit(solution)/shard_map/all_to_all | solution.py:414
  85.9 1.4 copy-start.1

commit v2 on v1

--- a/solution.py
+++ b/solution.py
@@ -67,6 +67,10 @@
     return dot(hh, xh) + dot(hh, xl) + dot(hl, xh)
 
 
+def together(count):
+    return max(k for k in range(1, 6) if count % k == 0)
+
+
 class Shape:
     def __init__(self, planes, gy, gz, devices):
         self.planes, self.gy, self.gz, self.devices = planes, gy, gz, devices
@@ -86,13 +90,18 @@
     hh = hh_ref[...]
     hl = hl_ref[...]
 
-    def plane(j, _):
-        xh, xl = split_bf16(source(j))
-        th, tl = split_bf16(right_transform(xh, xl, hh, hl))
-        f_ref[j] = left_transform(th, tl, hh, hl)
-        return 0
-
-    lax.fori_loop(0, sh.planes, plane, 0)
+    many = together(sh.planes)
+
+    def pair(i, _):
+        js = [i * many + k for k in range(many)]
+        src = [split_bf16(source(j)) for j in js]
+        right = [right_transform(xh, xl, hh, hl) for xh, xl in src]
+        parts = [split_bf16(x) for x in right]
+        for j, (th, tl) in zip(js, parts):
+            f_ref[j] = left_transform(th, tl, hh, hl)
+        return 0
+
+    lax.fori_loop(0, sh.planes // many, pair, 0)
 
     def group(g, _):
         row = pl.multiple_of(g * SUB, SUB)
@@ -296,12 +305,17 @@
     hh = hh_ref[...]
     hl = hl_ref[...]
 
-    def plane(j, _):
-        th, tl = split_bf16(right_transform(uh[j], ul[j], hh, hl))
-        m[j] = left_transform(th, tl, hh, hl)
-        return 0
-
-    lax.fori_loop(0, sh.planes + 2, plane, 0)
+    many = together(sh.planes + 2)
+
+    def pair(i, _):
+        js = [i * many + k for k in range(many)]
+        right = [right_transform(uh[j], ul[j], hh, hl) for j in js]
+        parts = [split_bf16(x) for x in right]
+        for j, (th, tl) in zip(js, parts):
+            m[j] = left_transform(th, tl, hh, hl)
+        return 0
+
+    lax.fori_loop(0, (sh.planes + 2) // many, pair, 0)
 
 
 def step_kernel(sh, stage, *refs):
@@ -406,7 +420,7 @@
         out_specs=[whole] * len(out_shapes),
         scratch_shapes=list(scratch),
         input_output_aliases=aliases or {},
-        compiler_params=pltpu.CompilerParams(vmem_limit_bytes=60 * 1024 * 1024),
+        compiler_params=pltpu.CompilerParams(vmem_limit_bytes=12 * 1024 * 1024),
     )(*operands)
 
 
@@ -428,25 +442,6 @@
     planes, gy, gz = potential.shape
     sh = Shape(planes, gy, gz, devices)
 
-    wide = conductivity.shape[1]
-    craw = lax.all_to_all(
-        conductivity.reshape(parts, planes, wide, gz), "py", split_axis=0, concat_axis=0, tiled=True
-    )
-    drive = (
-        excite_gain * potential * (potential - threshold) * (1.0 - potential) - potential * recovery
-    )
-    v_star = potential + time_step * (drive + stimulus)
-    rate = base_rate + rate_slope * recovery / (potential + rate_shift)
-    recovery_next = recovery + time_step * rate * (
-        -recovery - excite_gain * potential * (potential - threshold - 1.0)
-    )
-    ulo, uhi = neighbours(v_star[:1], v_star[-1:], AXES)
-
-    def edge(j):
-        return craw[:, j].reshape(1, gy, gz)
-
-    clo, chi = neighbours(edge(0), edge(planes - 1), AXES)
-
     rho, scale, block, closure = mode_tables(sh.gx, gy, gz, planes)
     groups = gy // SUB
 
@@ -464,6 +459,29 @@
     rho = jnp.asarray(rho.astype(np.float32))
     scale = jnp.asarray(scale.astype(np.float32))
     hh, hl = (jnp.asarray(x) for x in cas_parts(gy))
+
+    coef = jnp.zeros((SUB, gz), jnp.float32)
+    conductivity, block, closure, onward, coef = lax.optimization_barrier(
+        (conductivity, block, closure, onward, coef)
+    )
+    wide = conductivity.shape[1]
+    craw = lax.all_to_all(
+        conductivity.reshape(parts, planes, wide, gz), "py", split_axis=0, concat_axis=0, tiled=True
+    )
+    drive = (
+        excite_gain * potential * (potential - threshold) * (1.0 - potential) - potential * recovery
+    )
+    v_star = potential + time_step * (drive + stimulus)
+    rate = base_rate + rate_slope * recovery / (potential + rate_shift)
+    recovery_next = recovery + time_step * rate * (
+        -recovery - excite_gain * potential * (potential - threshold - 1.0)
+    )
+    ulo, uhi = neighbours(v_star[:1], v_star[-1:], AXES)
+
+    def edge(j):
+        return craw[:, j].reshape(1, gy, gz)
+
+    clo, chi = neighbours(edge(0), edge(planes - 1), AXES)
 
     slab = (planes, gy, gz)
     payload = (devices, sh.rows + SUB, LANE)
@@ -481,7 +499,6 @@
         pltpu.VMEM((planes + 2, gy, gz), jnp.bfloat16),
         pltpu.VMEM((planes + 2, gy, gz), jnp.float32),
     ]
-    coef = jnp.zeros((SUB, gz), jnp.float32)
     coefs = []
     basis = []
     z = w = s = q = t = None

time: 358 us -> 264 us (0.74)
  Pallas kernels: 134 us -> 45.4 us
  blocking collectives: 152 us -> 172 us
  waiting for transfers between devices: 38.2 us -> 20.9 us
  starting transfers between devices: 22 us -> 17 us
    pallas_call x10, Pallas kernels: 134 us -> 45.4 us  [call(): pl.pallas_call(kernel, name=name, out_shape=[jax.ShapeDtypeStruct(s, jnp....]
    all_to_all x8 -> x9, blocking collectives: 152 us -> 172 us  [exchange(): return lax.all_to_all(x, AXES, split_axis=0, concat_axis=0, tiled=True)]
    all_to_all x1 -> x0, waiting for transfers between devices: 16.6 us -> none  [exchange(): return lax.all_to_all(x, AXES, split_axis=0, concat_axis=0, tiled=True)]
    all_to_all x1 -> x0, starting transfers between devices: 5.01 us -> none  [exchange(): return lax.all_to_all(x, AXES, split_axis=0, concat_axis=0, tiled=True)]
  transfers between devices with their start and end apart: 6 -> 5, of which waited for: 3 -> 2; matrix products, arithmetic and copies ran while one was open for 2% -> 2% of each run, Pallas kernels for 0% -> 0%
where the time goes in v2:
time: 264 us; the launch traced here: 263 us
  blocking collectives  172 us (65%)
  Pallas kernels  45.4 us (17%)
  waiting for transfers between devices  20.9 us (8%)
  starting transfers between devices  17 us (6%)
  other arithmetic  4.55 us (2%)
    all_to_all x9, blocking collectives, exchange(): return lax.all_to_all(x, AXES, split_axis=0, concat_axis=0, tiled=True)  172 us
    pallas_call x10, Pallas kernels, call(): pl.pallas_call(kernel, name=name, out_shape=[jax.ShapeDtypeStruct(s, jnp....  45.4 us
    all_to_all x1, waiting for transfers between devices, local(): lax.all_to_all(conductivity.reshape(parts, planes, wide, gz), 'py', split...  16.8 us
    ppermute x2, starting transfers between devices, neighbours(): lax.ppermute(first, axes, [((i + 1) % count, i) for i in range(count)])  12.5 us
  transfers between devices with their start and end apart: 5, of which 2 were waited for; matrix products, arithmetic and copies ran while one was open for 2% of the time, Pallas kernels for 0%

profile of v2, /device:TPU:0, one launch (start us, length us, event | category | flops | bytes accessed | tf_op | source)
XLA Modules:
  0.0 263.3 jit_solution(8491259384326124867)
XLA Ops:
  0.7 0.7 dynamic-slice_bitcast_fusion.refs_1_
  1.4 0.1 broadcast_in_dim.4.refs_3_
  1.4 4.4 %all-to-all-start = ((f32[4,8,64,256]{3,2,1,0:T(8,128)}), f32[4,8,64,256]{3,2,1,0:T(8,128)}, u32[]{:S(2)}, u32[]{:S(2)}) async-start(f32[4,8,64,256]{3,2,1,0:T(8,128)} %bitcast.5), calls=%async_computation | async-start | bytes 4194304 | tf_op jit(solution)/shard_map/all_to_all | solution.py:468
  5.9 4.5 %multiply_add_fusion = (f32[8,256,256]{2,1,0:T(8,128)}, f32[8,256,256]{2,1,0:T(8,128)S(1)}) fusion(f32[8,256,256]{2,1,0:T(8,128)} %param.11, f32[8,256,256]{2,1,0:T(8,128)} %param.10, f32[8,256,256]{2,1,0:T(8,128)} %param.12), kind=kLoop, calls=%fused_computation | loop fusion | flops 11010048 | bytes 10485760 | tf_op jit(solution)/shard_map/add | solution.py:476
  10.4 0.0 copy-start
  10.4 0.0 copy-start.2
  10.4 0.0 copy-start.3
  10.4 0.7 fusion.3
  11.2 7.1 %collective-permute-start.1 = (f32[1,256,256]{2,1,0:T(8,128)}, f32[1,256,256]{2,1,0:T(8,128)S(1)}, u32[]{:S(2)}, u32[]{:S(2)}) collective-permute-start(f32[1,256,256]{2,1,0:T(8,128)} %get-tuple-element.82), channel_id=1, source_target_pairs={{1,0},{2,1},{3,2},{4,3},{5,4},{6,5},{7,6},{8,7},{9,8},{10,9},{11,1... | collective-permute-start | bytes 786440 | tf_op jit(solution)/shard_map/ppermute | solution.py:435
  18.3 0.0 collective-permute-start
  18.3 16.8 %all-to-all-done.craw = f32[4,8,64,256]{3,2,1,0:T(8,128)} async-done(((f32[4,8,64,256]{3,2,1,0:T(8,128)}), f32[4,8,64,256]{3,2,1,0:T(8,128)}, u32[]{:S(2)}, u32[]{:S(2)}) %all-to-all-start) | async-done | bytes 2097184 | tf_op jit(solution)/shard_map/all_to_all | solution.py:468
  35.2 1.1 fusion.2
  36.2 0.1 collective-permute-start.2
  36.3 5.3 %collective-permute-start.3 = (f32[1,256,256]{2,1,0:T(8,128)S(1)}, f32[1,256,256]{2,1,0:T(8,128)S(1)}, u32[]{:S(2)}, u32[]{:S(2)}) collective-permute-start(f32[1,256,256]{2,1,0:T(8,128)S(1)} %bitcast.6), channel_id=1, source_target_pairs={{1,0},{2,1},{3,2},{4,3},{5,4},{6,5},{7,6},{8,7},{9,8},{10,9},{11,1... | collective-permute-start | bytes 786440 | tf_op jit(solution)/shard_map/ppermute | solution.py:435
  41.6 0.0 collective-permute-done.1.uhi
  41.6 0.0 collective-permute-done.ulo
  41.6 4.0 %collective-permute-done.2.clo = f32[1,256,256]{2,1,0:T(8,128)S(1)} collective-permute-done((f32[1,256,256]{2,1,0:T(8,128)S(1)}, f32[1,256,256]{2,1,0:T(8,128)S(1)}, u32[]{:S(2)}, u32[]{:S(2)}) %collective-permute-start.2) | collective-permute-done | bytes 262176 | tf_op jit(solution)/shard_map/ppermute | solution.py:434
  45.7 0.0 collective-permute-done.3.chi
  45.7 0.0 copy-done
  45.7 0.0 copy-done.2
  45.7 0.0 copy-done.3
  45.7 8.0 %start.1 = (f32[9,256,256]{2,1,0:T(8,128)S(1)}, f32[8,256,256]{2,1,0:T(8,128)S(1)}, f32[8,256,256]{2,1,0:T(8,128)S(1)}, f32[8,256,256]{2,1,0:T(8,128)S(1)}, f32[...) custom-call(f32[8,256,256]{2,1,0:T(8,128)S(1)} %get-tuple-element.79.u.refs_4_, ...), custom_call_target="tpu_custom_call" | custom-call | tf_op jit(solution)/shard_map/start/pallas_call | solution.py:415
  53.7 0.0 copy-start.1
  53.7 23.5 %all_to_all.50.refs_0_ = f32[32,40,128]{2,1,0:T(8,128)S(1)} all-to-all(f32[32,40,128]{2,1,0:T(8,128)S(1)} %get-tuple-element.42), channel_id=1, replica_groups=mesh['px'=8,'py'=4] {'px','py'}, dimensions={0} | all-to-all | bytes 1310720 | tf_op jit(solution)/shard_map/all_to_all | solution.py:428
  77.2 0.3 scan0.1
  77.5 18.8 %all_to_all.51.refs_1_ = f32[32,32,128]{2,1,0:T(8,128)S(1)} all-to-all(f32[32,32,128]{2,1,0:T(8,128)S(1)} %scan0.1), channel_id=1, replica_groups=mesh['px'=8,'py'=4] {'px','py'}, dimensions={0} | all-to-all | bytes 1048576 | tf_op jit(solution)/shard_map/all_to_all | solution.py:428
  96.3 0.0 copy-done.1
  96.3 8.4 %step0.1 = (f32[8,256,256]{2,1,0:T(8,128)S(1)}, f32[8,256,256]{2,1,0:T(8,128)S(1)}, f32[8,256,256]{2,1,0:T(8,128)S(1)}, f32[32,40,128]{2,1,0:T(8,128)S(1)}) custom-call(f32[8,256,256]{2,1,0:T(8,128)S(1)} %get-tuple-element.41.refs_0_, f32[32,32,128]{2,1,0:T(8,128)S(1)} %all_to_all.51.refs_1_, f32[256,256]{1,0:T(8,128)S(1)} %copy-done, ...), custom_call_target="tpu_custom_call" | custom-call | tf_op jit(solution)/shard_map/step0/pallas_call | solution.py:415
  104.7 20.8 %all_to_all.52.refs_0_ = f32[32,40,128]{2,1,0:T(8,128)S(1)} all-to-all(f32[32,40,128]{2,1,0:T(8,128)S(1)} %get-tuple-element.50), channel_id=1, replica_groups=mesh['px'=8,'py'=4] {'px','py'}, dimensions={0} | all-to-all | bytes 1310720 | tf_op jit(solution)/shard_map/all_to_all | solution.py:428
  125.5 0.4 scan1.1
  125.9 18.8 %all_to_all.53.refs_1_ = f32[32,32,128]{2,1,0:T(8,128)S(1)} all-to-all(f32[32,32,128]{2,1,0:T(8,128)S(1)} %get-tuple-element.54), channel_id=1, replica_groups=mesh['px'=8,'py'=4] {'px','py'}, dimensions={0} | all-to-all | bytes 1048576 | tf_op jit(solution)/shard_map/all_to_all | solution.py:428
  144.8 9.0 %step1.1 = (f32[8,256,256]{2,1,0:T(8,128)S(1)}, f32[8,256,256]{2,1,0:T(8,128)S(1)}, f32[8,256,256]{2,1,0:T(8,128)S(1)}, f32[8,256,256]{2,1,0:T(8,128)S(1)}, f32[...) custom-call(f32[8,256,256]{2,1,0:T(8,128)S(1)} %get-tuple-element.53.refs_0_, ...), custom_call_target="tpu_custom_call" | custom-call | tf_op jit(solution)/shard_map/step1/pallas_call | solution.py:415
  153.8 20.8 %all_to_all.54.refs_0_ = f32[32,40,128]{2,1,0:T(8,128)S(1)} all-to-all(f32[32,40,128]{2,1,0:T(8,128)S(1)} %get-tuple-element.57), channel_id=1, replica_groups=mesh['px'=8,'py'=4] {'px','py'}, dimensions={0} | all-to-all | bytes 1310720 | tf_op jit(solution)/shard_map/all_to_all | solution.py:428
  174.6 0.4 scan2.1
  175.0 18.8 %all_to_all.55.refs_1_ = f32[32,32,128]{2,1,0:T(8,128)S(1)} all-to-all(f32[32,32,128]{2,1,0:T(8,128)S(1)} %get-tuple-element.60), channel_id=1, replica_groups=mesh['px'=8,'py'=4] {'px','py'}, dimensions={0} | all-to-all | bytes 1048576 | tf_op jit(solution)/shard_map/all_to_all | solution.py:428
  193.8 9.5 %step2.1 = (f32[8,256,256]{2,1,0:T(8,128)S(1)}, f32[8,256,256]{2,1,0:T(8,128)S(1)}, f32[8,256,256]{2,1,0:T(8,128)S(1)}, f32[8,256,256]{2,1,0:T(8,128)S(1)}, f32[...) custom-call(f32[8,256,256]{2,1,0:T(8,128)S(1)} %get-tuple-element.59, ...), custom_call_target="tpu_custom_call" | custom-call | tf_op jit(solution)/shard_map/step2/pallas_call | solution.py:415
  203.4 20.8 %all_to_all.56.refs_0_ = f32[32,40,128]{2,1,0:T(8,128)S(1)} all-to-all(f32[32,40,128]{2,1,0:T(8,128)S(1)} %get-tuple-element.66), channel_id=1, replica_groups=mesh['px'=8,'py'=4] {'px','py'}, dimensions={0} | all-to-all | bytes 1310720 | tf_op jit(solution)/shard_map/all_to_all | solution.py:428
  224.1 0.4 scan3.1
  224.6 18.8 %all_to_all.57.refs_1_ = f32[32,32,128]{2,1,0:T(8,128)S(1)} all-to-all(f32[32,32,128]{2,1,0:T(8,128)S(1)} %get-tuple-element.69), channel_id=1, replica_groups=mesh['px'=8,'py'=4] {'px','py'}, dimensions={0} | all-to-all | bytes 1048576 | tf_op jit(solution)/shard_map/all_to_all | solution.py:428
  243.4 6.7 %step3.1 = (f32[8,256,256]{2,1,0:T(8,128)S(1)}, f32[32,8,128]{2,1,0:T(8,128)S(1)}) custom-call(f32[8,256,256]{2,1,0:T(8,128)S(1)} %get-tuple-element.68.refs_0_, f32[32,32,128]{2,1,0:T(8,128)S(1)} %all_to_all.57.refs_1_, f32[256,256]{1,0:T(8,128)S(1)} %copy-done, f32[256,256]{1,0:T(8,128)S(1)} %copy-done.1, bf16[256,256]{1,0:T(8,128)(2,1)S(1)} %copy-done.3, ...), custom_call_target="tpu_custom_call" | custom-call | tf_op jit(solution)/shard_map/step3/pallas_call | solution.py:415
  250.1 11.0 %all_to_all.58.refs_3_ = f32[32,8,128]{2,1,0:T(8,128)S(1)} all-to-all(f32[32,8,128]{2,1,0:T(8,128)S(1)} %get-tuple-element.76), channel_id=1, replica_groups=mesh['px'=8,'py'=4] {'px','py'}, dimensions={0} | all-to-all | bytes 262144 | tf_op jit(solution)/shard_map/all_to_all | solution.py:428
  261.1 2.2 finish.1
  (3 shorter events, 0.0 us)
Async XLA Ops:
  1.4 33.7 %all-to-all-start = ((f32[4,8,64,256]{3,2,1,0:T(8,128)}), f32[4,8,64,256]{3,2,1,0:T(8,128)}, u32[]{:S(2)}, u32[]{:S(2)}) async-start(f32[4,8,64,256]{3,2,1,0:T(8,128)} %bitcast.5), calls=%async_computation | async-start | bytes 4194304 | tf_op jit(solution)/shard_map/all_to_all | solution.py:468
  10.4 35.2 %copy-start = (f32[256,256]{1,0:T(8,128)S(1)}, f32[256,256]{1,0:T(8,128)}, u32[]{:S(2)}) copy-start(f32[256,256]{1,0:T(8,128)} %constant.83.clone.rho.refs_2_) | copy-start | bytes 786436
  10.4 35.2 %copy-start.2 = (bf16[256,256]{1,0:T(8,128)(2,1)S(1)}, bf16[256,256]{1,0:T(8,128)(2,1)}, u32[]{:S(2)}) copy-start(bf16[256,256]{1,0:T(8,128)(2,1)} %constant.86.clone.hl.refs_5_) | copy-start | bytes 393220
  10.4 35.3 %copy-start.3 = (bf16[256,256]{1,0:T(8,128)(2,1)S(1)}, bf16[256,256]{1,0:T(8,128)(2,1)}, u32[]{:S(2)}) copy-start(bf16[256,256]{1,0:T(8,128)(2,1)} %constant.85.clone.hh.refs_4_) | copy-start | bytes 393220
  11.2 30.4 %collective-permute-start.1 = (f32[1,256,256]{2,1,0:T(8,128)}, f32[1,256,256]{2,1,0:T(8,128)S(1)}, u32[]{:S(2)}, u32[]{:S(2)}) collective-permute-start(f32[1,256,256]{2,1,0:T(8,128)} %get-tuple-element.82), channel_id=1, source_target_pairs={{1,0},{2,1},{3,2},{4,3},{5,4},{6,5},{7,6},{8,7},{9,8},{10,9},{11,1... | collective-permute-start | bytes 786440 | tf_op jit(solution)/shard_map/ppermute | solution.py:435
  18.3 23.3 %collective-permute-start = (f32[1,256,256]{2,1,0:T(8,128)S(1)}, f32[1,256,256]{2,1,0:T(8,128)S(1)}, u32[]{:S(2)}, u32[]{:S(2)}) collective-permute-start(f32[1,256,256]{2,1,0:T(8,128)S(1)} %get-tuple-element.83), channel_id=1, source_target_pairs={{0,1},{1,2},{2,3},{3,4},{4,5},{5,6},{6,7},{7,8},{8,9},{9,10},{10,1... | collective-permute-start | bytes 786440 | tf_op jit(solution)/shard_map/ppermute | solution.py:434
  36.2 9.4 %collective-permute-start.2 = (f32[1,256,256]{2,1,0:T(8,128)S(1)}, f32[1,256,256]{2,1,0:T(8,128)S(1)}, u32[]{:S(2)}, u32[]{:S(2)}) collective-permute-start(f32[1,256,256]{2,1,0:T(8,128)S(1)} %bitcast.7), channel_id=1, source_target_pairs={{0,1},{1,2},{2,3},{3,4},{4,5},{5,6},{6,7},{7,8},{8,9},{9,10},{10,1... | collective-permute-start | bytes 786440 | tf_op jit(solution)/shard_map/ppermute | solution.py:434
  36.3 9.4 %collective-permute-start.3 = (f32[1,256,256]{2,1,0:T(8,128)S(1)}, f32[1,256,256]{2,1,0:T(8,128)S(1)}, u32[]{:S(2)}, u32[]{:S(2)}) collective-permute-start(f32[1,256,256]{2,1,0:T(8,128)S(1)} %bitcast.6), channel_id=1, source_target_pairs={{1,0},{2,1},{3,2},{4,3},{5,4},{6,5},{7,6},{8,7},{9,8},{10,9},{11,1... | collective-permute-start | bytes 786440 | tf_op jit(solution)/shard_map/ppermute | solution.py:435
  53.7 42.6 %copy-start.1 = (f32[256,256]{1,0:T(8,128)S(1)}, f32[256,256]{1,0:T(8,128)}, u32[]{:S(2)}) copy-start(f32[256,256]{1,0:T(8,128)} %constant.84.clone.refs_3_) | copy-start | bytes 786436

commit v3 on v2

--- a/solution.py
+++ b/solution.py
@@ -75,18 +75,24 @@
     def __init__(self, planes, gy, gz, devices):
         self.planes, self.gy, self.gz, self.devices = planes, gy, gz, devices
         self.gx = planes * devices
+        self.chips = devices // 2
         self.halves = gz // LANE
         self.per_group = 2 * self.halves
-        self.slots = gy // SUB * self.per_group // devices
+        self.groups = gy // SUB // 2
+        self.tiles = self.groups * self.per_group
+        self.slots = self.tiles // self.chips
         assert self.per_group % self.slots == 0
         self.rows = self.slots * SUB
+
+    def tile(self, group, kind, half):
+        return group * self.per_group + kind * self.halves + half
 
     def place(self, group, kind, half):
         q = kind * self.halves + half
         return group * (self.per_group // self.slots) + q // self.slots, q % self.slots * SUB
 
 
-def emit_forward(sh, source, rho, hh_ref, hl_ref, f_ref, pay_ref, scal):
+def emit_forward(sh, source, core, rho, hh_ref, hl_ref, f_ref, keep_ref, send_ref, scal):
     hh = hh_ref[...]
     hl = hl_ref[...]
 
@@ -103,29 +109,79 @@
 
     lax.fori_loop(0, sh.planes // many, pair, 0)
 
+    for side, ref in ((core, keep_ref), (1 - core, send_ref)):
+
+        def group(g, _, side=side, ref=ref):
+            row = pl.multiple_of((side * sh.groups + g) * SUB, SUB)
+            for half in range(sh.halves):
+                lanes = slice(half * LANE, (half + 1) * LANE)
+                decay = rho[pl.ds(row, SUB), lanes]
+                f = [f_ref[j, pl.ds(row, SUB), lanes] for j in range(sh.planes)]
+                p = f[0]
+                e = f[-1]
+                for j in range(1, sh.planes):
+                    p = f[j] + decay * p
+                    e = f[sh.planes - 1 - j] + decay * e
+                ref[sh.tile(g, 0, half)] = p
+                ref[sh.tile(g, 1, half)] = e
+            return 0
+
+        lax.fori_loop(0, sh.groups, group, 0, unroll=2)
+        ref[sh.tiles] = scal
+
+
+def join_kernel(sh, core_ref, keep, other, block, out):
+    core = core_ref[0]
+    early = core == 0
+    scal = keep[sh.tiles] + other[sh.tiles]
+
     def group(g, _):
-        row = pl.multiple_of(g * SUB, SUB)
+        row = pl.multiple_of((core * sh.groups + g) * SUB, SUB)
         for half in range(sh.halves):
-            lanes = slice(half * LANE, (half + 1) * LANE)
-            decay = rho[pl.ds(row, SUB), lanes]
-            f = [f_ref[j, pl.ds(row, SUB), lanes] for j in range(sh.planes)]
-            p = f[0]
-            e = f[-1]
-            for j in range(1, sh.planes):
-                p = f[j] + decay * p
-                e = f[sh.planes - 1 - j] + decay * e
-            for kind, value in ((0, p), (1, e)):
-                d, at = sh.place(g, kind, half)
-                pay_ref[d, pl.ds(at, SUB), :] = value
-        return 0
-
-    lax.fori_loop(0, sh.gy // SUB, group, 0)
+            a = block[pl.ds(row, SUB), half * LANE : (half + 1) * LANE]
+            for kind in range(2):
+                at = sh.tile(g, kind, half)
+                mine, its = keep[at], other[at]
+                first = jnp.where(early, mine, its)
+                second = jnp.where(early, its, mine)
+                d, to = sh.place(g, kind, half)
+                value = a * first + second if kind == 0 else first + a * second
+                out[d, pl.ds(to, SUB), :] = value
+        return 0
+
+    lax.fori_loop(0, sh.groups, group, 0, unroll=4)
 
     def spread(d, _):
-        pay_ref[d, pl.ds(sh.rows, SUB), :] = scal
-        return 0
-
-    lax.fori_loop(0, sh.devices, spread, 0)
+        out[d, pl.ds(sh.rows, SUB), :] = scal
+        return 0
+
+    lax.fori_loop(0, sh.chips, spread, 0, unroll=4)
+
+
+def part_kernel(sh, core_ref, carry, keep, other, block, own, send):
+    core = core_ref[0]
+    early = core == 0
+
+    def group(g, _):
+        row = pl.multiple_of((core * sh.groups + g) * SUB, SUB)
+        for half in range(sh.halves):
+            a = block[pl.ds(row, SUB), half * LANE : (half + 1) * LANE]
+            for kind in range(2):
+                at = sh.tile(g, kind, half)
+                mine, its = keep[at], other[at]
+                d, to = sh.place(g, kind, half)
+                outer = carry[d, pl.ds(to, SUB), :]
+                if kind == 0:
+                    inner = jnp.where(early, mine, its) + a * outer
+                    own[at] = jnp.where(early, outer, inner)
+                    send[at] = jnp.where(early, inner, outer)
+                else:
+                    inner = jnp.where(early, its, mine) + a * outer
+                    own[at] = jnp.where(early, inner, outer)
+                    send[at] = jnp.where(early, outer, inner)
+        return 0
+
+    lax.fori_loop(0, sh.groups, group, 0, unroll=4)
 
 
 def stencil(sh, j, here, before, after, gx_ref, gy_ref, gz_ref):
@@ -153,7 +209,7 @@
 
 
 def start_kernel(
-    sh, parts, u, ulo, uhi, craw, clo, chi, rho, hh, hl, gx, gy, gz, r, f, pay, c
+    sh, parts, core_ref, u, ulo, uhi, craw, clo, chi, rho, hh, hl, gx, gy, gz, r, f, keep, send, c
 ):
     wide = sh.gy // parts
     for k in range(parts):
@@ -184,9 +240,8 @@
 
     lax.fori_loop(1, last, inner, 0)
     r[last] = -stencil(sh, last, u[last], u[last - 1], uhi[0], gx, gy, gz)
-    emit_forward(
-        sh, lambda j: r[j], rho, hh, hl, f, pay, jnp.zeros((SUB, LANE), jnp.float32)
-    )
+    scal = jnp.zeros((SUB, LANE), jnp.float32)
+    emit_forward(sh, lambda j: r[j], core_ref[0], rho, hh, hl, f, keep, send, scal)
 
 
 def scan_kernel(sh, first, *refs):
@@ -195,7 +250,7 @@
         (out,) = refs[4:]
     else:
         coef, out, coef_out = refs[4:]
-    count = sh.devices
+    count = sh.chips
 
     def run(rows, forward, store):
         a = decay[rows]
@@ -235,7 +290,7 @@
         run(rows, False, store_backward)
 
     if not first:
-        sums = sum_rows(sh.devices, recv, sh.rows)
+        sums = sum_rows(sh.chips, recv, sh.rows)
         coef_out[...] = next_coefficients(sums, coef[...], sh.gz)
 
 
@@ -264,44 +319,43 @@
     )
 
 
-def emit_inverse(sh, f, carry, rho, scale, hh_ref, hl_ref, uh, ul, m):
+def emit_inverse(sh, core, f, own, other, rho, scale, hh_ref, hl_ref, uh, ul, m):
     tall = 2 * SUB
-
-    def group(i, _):
-        row = pl.multiple_of(i * tall, tall)
-        for half in range(sh.halves):
-            lanes = slice(half * LANE, (half + 1) * LANE)
-            decay = rho[pl.ds(row, tall), lanes]
-            gain = scale[pl.ds(row, tall), lanes]
-            ends = []
-            for kind in range(2):
-                tiles = []
-                for g in (2 * i, 2 * i + 1):
-                    d, at = sh.place(g, kind, half)
-                    tiles.append(carry[d, pl.ds(at, SUB), :])
-                ends.append(jnp.concatenate(tiles, axis=0))
-            first, final = ends
-
-            def put(j, value):
-                high, low = split_bf16(gain * value)
-                uh[j, pl.ds(row, tall), lanes] = high
-                ul[j, pl.ds(row, tall), lanes] = low
-
-            fields = [f[j, pl.ds(row, tall), lanes] for j in range(sh.planes)]
-            back = [None] * sh.planes
-            e = final
-            for j in reversed(range(sh.planes)):
-                back[j] = decay * e
-                e = fields[j] + back[j]
-            put(0, first + decay * e)
-            p = first
-            for j in range(sh.planes):
-                p = fields[j] + decay * p
-                put(j + 1, p + back[j])
-            put(sh.planes + 1, decay * p + final)
-        return 0
-
-    lax.fori_loop(0, sh.gy // tall, group, 0)
+    for side, carry in ((core, own), (1 - core, other)):
+
+        def group(i, _, side=side, carry=carry):
+            row = pl.multiple_of(side * (sh.groups * SUB) + i * tall, tall)
+            for half in range(sh.halves):
+                lanes = slice(half * LANE, (half + 1) * LANE)
+                decay = rho[pl.ds(row, tall), lanes]
+                gain = scale[pl.ds(row, tall), lanes]
+                first, final = (
+                    jnp.concatenate(
+                        [carry[sh.tile(g, kind, half)] for g in (2 * i, 2 * i + 1)], axis=0
+                    )
+                    for kind in range(2)
+                )
+
+                def put(j, value):
+                    high, low = split_bf16(gain * value)
+                    uh[j, pl.ds(row, tall), lanes] = high
+                    ul[j, pl.ds(row, tall), lanes] = low
+
+                fields = [f[j, pl.ds(row, tall), lanes] for j in range(sh.planes)]
+                back = [None] * sh.planes
+                e = final
+                for j in reversed(range(sh.planes)):
+                    back[j] = decay * e
+                    e = fields[j] + back[j]
+                put(0, first + decay * e)
+                p = first
+                for j in range(sh.planes):
+                    p = fields[j] + decay * p
+                    put(j + 1, p + back[j])
+                put(sh.planes + 1, decay * p + final)
+            return 0
+
+        lax.fori_loop(0, sh.groups // 2, group, 0)
     hh = hh_ref[...]
     hl = hl_ref[...]
 
@@ -319,7 +373,7 @@
 
 
 def step_kernel(sh, stage, *refs):
-    names = ["f", "carry", "rho", "scale", "hh", "hl", "gx", "gy", "gz", "r"]
+    names = ["core", "f", "own", "other", "rho", "scale", "hh", "hl", "gx", "gy", "gz", "r"]
     if stage > 0:
         names += ["coef", "z", "w"]
     if stage > 1:
@@ -333,13 +387,13 @@
         outs = ["z_new", "w_new", "r_new", "s_new", "q_new", "t_new"]
         if stage == 1:
             outs.remove("s_new")
-    outs += ["pay"] if last else ["f_new", "pay"]
+    outs += ["pay"] if last else ["f_new", "keep", "send"]
     scratch = ["uh", "ul", "m"]
-    if last:
-        scratch += []
     k = dict(zip(names + outs + scratch, refs, strict=True))
     m = k["m"]
-    emit_inverse(sh, k["f"], k["carry"], k["rho"], k["scale"], k["hh"], k["hl"], k["uh"], k["ul"], m)
+    core = k["core"][0]
+    tables = (k["rho"], k["scale"], k["hh"], k["hl"])
+    emit_inverse(sh, core, k["f"], k["own"], k["other"], *tables, k["uh"], k["ul"], m)
     if stage > 0:
         alpha = k["coef"][1:2, :]
         beta = k["coef"][2:3, :]
@@ -383,7 +437,8 @@
         lax.fori_loop(0, sh.devices, spread, 0)
     else:
         w_new = k["w_new"]
-        emit_forward(sh, lambda j: w_new[j], k["rho"], k["hh"], k["hl"], k["f_new"], k["pay"], scal)
+        into = (k["f_new"], k["keep"], k["send"])
+        emit_forward(sh, lambda j: w_new[j], core, k["rho"], k["hh"], k["hl"], *into, scal)
 
 
 def finish_kernel(sh, *refs):
@@ -416,7 +471,10 @@
         kernel,
         name=name,
         out_shape=[jax.ShapeDtypeStruct(s, jnp.float32) for s in out_shapes],
-        in_specs=[whole] * len(operands),
+        in_specs=[
+            pl.BlockSpec(memory_space=pltpu.MemorySpace.SMEM) if x.dtype == jnp.int32 else whole
+            for x in operands
+        ],
         out_specs=[whole] * len(out_shapes),
         scratch_shapes=list(scratch),
         input_output_aliases=aliases or {},
@@ -424,8 +482,10 @@
     )(*operands)
 
 
-def exchange(x):
-    return lax.all_to_all(x, AXES, split_axis=0, concat_axis=0, tiled=True)
+def exchange(x, groups=None):
+    return lax.all_to_all(
+        x, AXES, split_axis=0, concat_axis=0, tiled=True, axis_index_groups=groups
+    )
 
 
 def neighbours(first, final, axes):
@@ -447,12 +507,15 @@
 
     def own_tiles(table):
         tiles = table.astype(np.float32).reshape(groups, SUB, sh.halves, LANE).transpose(0, 2, 1, 3)
-        both = np.concatenate([tiles, tiles], axis=1).reshape(devices, sh.rows, LANE)
+        both = np.concatenate([tiles, tiles], axis=1).reshape(2, sh.chips, sh.rows, LANE)
+        both = both.transpose(1, 0, 2, 3).reshape(devices, sh.rows, LANE)
         return lax.dynamic_index_in_dim(jnp.asarray(both), lax.axis_index(AXES), 0, False)
 
-    block = own_tiles(block)
+    across = jnp.asarray(block.astype(np.float32))
+    block = own_tiles(block * block)
     closure = own_tiles(closure)
-    slot = lax.axis_index(AXES) * sh.slots + jnp.arange(sh.rows, dtype=jnp.int32)[:, None] // SUB
+    core = jnp.reshape(lax.axis_index(AXES) % 2, (1,))
+    slot = lax.axis_index(AXES) // 2 * sh.slots + jnp.arange(sh.rows, dtype=jnp.int32)[:, None] // SUB
     onward = jnp.broadcast_to(
         (slot % sh.per_group < sh.halves).astype(jnp.float32), (sh.rows, LANE)
     )
@@ -461,8 +524,8 @@
     hh, hl = (jnp.asarray(x) for x in cas_parts(gy))
 
     coef = jnp.zeros((SUB, gz), jnp.float32)
-    conductivity, block, closure, onward, coef = lax.optimization_barrier(
-        (conductivity, block, closure, onward, coef)
+    conductivity, block, closure, onward, coef, core = lax.optimization_barrier(
+        (conductivity, block, closure, onward, coef, core)
     )
     wide = conductivity.shape[1]
     craw = lax.all_to_all(
@@ -484,14 +547,18 @@
     clo, chi = neighbours(edge(0), edge(planes - 1), AXES)
 
     slab = (planes, gy, gz)
-    payload = (devices, sh.rows + SUB, LANE)
-    carries = (devices, sh.rows, LANE)
+    payload = (sh.chips, sh.rows + SUB, LANE)
+    carries = (sh.chips, sh.rows, LANE)
+    sums = (sh.tiles + 1, SUB, LANE)
+    parted = (sh.tiles, SUB, LANE)
+    swap = [(i, i ^ 1) for i in range(devices)]
+    same_core = [[2 * chip + side for chip in range(sh.chips)] for side in range(2)]
     tables = [rho, hh, hl]
-    gxf, gyf, gzf, r, f, pay = call(
+    gxf, gyf, gzf, r, f, keep, send = call(
         functools.partial(start_kernel, sh, parts),
         "start",
-        [(planes + 1, gy, gz), slab, slab, slab, slab, payload],
-        [v_star, ulo, uhi, craw, clo, chi] + tables,
+        [(planes + 1, gy, gz), slab, slab, slab, slab, sums, sums],
+        [core, v_star, ulo, uhi, craw, clo, chi] + tables,
         [pltpu.VMEM(slab, jnp.float32)],
     )
     spectral = [
@@ -503,7 +570,11 @@
     basis = []
     z = w = s = q = t = None
     for stage in range(ITERS):
-        recv = exchange(pay)
+        other = lax.ppermute(send, AXES, swap)
+        (pay,) = call(
+            functools.partial(join_kernel, sh), f"join{stage}", [payload], [core, keep, other, across]
+        )
+        recv = exchange(pay, same_core)
         if stage == 0:
             (carry,) = call(
                 functools.partial(scan_kernel, sh, True),
@@ -519,24 +590,32 @@
                 [recv, block, closure, onward, coef],
             )
             coefs.append(coef)
-        carry = exchange(carry)
-        operands = [f, carry, rho, scale, hh, hl, gxf, gyf, gzf, r]
+        carry = exchange(carry, same_core)
+        own, send = call(
+            functools.partial(part_kernel, sh),
+            f"part{stage}",
+            [parted, parted],
+            [core, carry, keep, other, across],
+        )
+        other = lax.ppermute(send, AXES, swap)
+        operands = [core, f, own, other, rho, scale, hh, hl, gxf, gyf, gzf, r]
         if stage > 0:
             operands += [coef, z, w]
         if stage > 1:
             operands += [s, q, t]
         kernel = functools.partial(step_kernel, sh, stage)
         if stage == 0:
-            z, w, f, pay = call(kernel, "step0", [slab, slab, slab, payload], operands, spectral)
+            shapes = [slab, slab, slab, sums, sums]
+            z, w, f, keep, send = call(kernel, "step0", shapes, operands, spectral)
         elif stage < ITERS - 1:
-            shapes = [slab] * (5 if stage == 1 else 6) + [slab, payload]
+            shapes = [slab] * (5 if stage == 1 else 6) + [slab, sums, sums]
             old_w = w
             results = call(kernel, f"step{stage}", shapes, operands, spectral)
             if stage == 1:
-                z, w, r, q, t, f, pay = results
+                z, w, r, q, t, f, keep, send = results
                 s = old_w
             else:
-                z, w, r, s, q, t, f, pay = results
+                z, w, r, s, q, t, f, keep, send = results
         else:
             z, pay = call(kernel, f"step{stage}", [slab, (devices, SUB, LANE)], operands, spectral)
         basis.append(z)

time: 264 us -> 230 us (0.87)
  blocking collectives: 172 us -> 125 us
  waiting for transfers between devices: 20.9 us -> 32.7 us
    all_to_all x9, blocking collectives: 172 us -> 125 us  [exchange(): lax.all_to_all(x, AXES, split_axis=0, concat_axis=0, tiled=True, axis_ind...]
    ppermute x0 -> x8, waiting for transfers between devices: none -> 11.8 us  [local(): other = lax.ppermute(send, AXES, swap)]
    pallas_call x10 -> x18, Pallas kernels: 45.4 us -> 45.9 us  [call(): pl.pallas_call(kernel, name=name, out_shape=[jax.ShapeDtypeStruct(s, jnp....]
  transfers between devices with their start and end apart: 5 -> 13, of which waited for: 2 -> 10; matrix products, arithmetic and copies ran while one was open for 2% -> 3% of each run, Pallas kernels for 0% -> 0%
where the time goes in v3:
time: 230 us; the launch traced here: 229 us
  blocking collectives  125 us (54%)
  Pallas kernels  45.9 us (20%)
  waiting for transfers between devices  32.7 us (14%)
  starting transfers between devices  17.9 us (8%)
  other arithmetic  4.55 us (2%)
  local copies, waits for them, and re-layouts  2.63 us (1%)
    all_to_all x9, blocking collectives, exchange(): lax.all_to_all(x, AXES, split_axis=0, concat_axis=0, tiled=True, axis_ind...  125 us
    pallas_call x18, Pallas kernels, call(): pl.pallas_call(kernel, name=name, out_shape=[jax.ShapeDtypeStruct(s, jnp....  45.9 us
    all_to_all x1, waiting for transfers between devices, local(): lax.all_to_all(conductivity.reshape(parts, planes, wide, gz), 'py', split...  16.8 us
    ppermute x2, starting transfers between devices, neighbours(): lax.ppermute(first, axes, [((i + 1) % count, i) for i in range(count)])  12.4 us
    ppermute x8, waiting for transfers between devices, local(): other = lax.ppermute(send, AXES, swap)  11.8 us
  transfers between devices with their start and end apart: 13, of which 10 were waited for; matrix products, arithmetic and copies ran while one was open for 3% of the time, Pallas kernels for 0%

profile of v3, /device:TPU:0, one launch (start us, length us, event | category | flops | bytes accessed | tf_op | source)
XLA Modules:
  0.0 229.2 jit_solution(2259836765456243891)
XLA Ops:
  0.7 0.7 dynamic-slice_bitcast_fusion.refs_1_
  1.4 0.1 broadcast_in_dim.4.refs_3_
  1.5 4.4 %all-to-all-start = ((f32[4,8,64,256]{3,2,1,0:T(8,128)}), f32[4,8,64,256]{3,2,1,0:T(8,128)}, u32[]{:S(2)}, u32[]{:S(2)}) async-start(f32[4,8,64,256]{3,2,1,0:T(8,128)} %bitcast.6), calls=%async_computation | async-start | bytes 4194304 | tf_op jit(solution)/shard_map/all_to_all | solution.py:531
  5.9 4.5 %multiply_add_fusion = (f32[8,256,256]{2,1,0:T(8,128)}, f32[8,256,256]{2,1,0:T(8,128)S(1)}) fusion(f32[8,256,256]{2,1,0:T(8,128)} %param.12, f32[8,256,256]{2,1,0:T(8,128)} %param.11, f32[8,256,256]{2,1,0:T(8,128)} %param.13), kind=kLoop, calls=%fused_computation | loop fusion | flops 11010048 | bytes 10485760 | tf_op jit(solution)/shard_map/add | solution.py:539
  10.5 0.7 fusion.3
  11.2 7.1 %collective-permute-start.1 = (f32[1,256,256]{2,1,0:T(8,128)}, f32[1,256,256]{2,1,0:T(8,128)S(1)}, u32[]{:S(2)}, u32[]{:S(2)}) collective-permute-start(f32[1,256,256]{2,1,0:T(8,128)} %get-tuple-element.108), channel_id=1, source_target_pairs={{1,0},{2,1},{3,2},{4,3},{5,4},{6,5},{7,6},{8,7},{9,8},{10,9},{11,1... | collective-permute-start | bytes 786440 | tf_op jit(solution)/shard_map/ppermute | solution.py:495
  18.3 0.0 collective-permute-start
  18.3 16.8 %all-to-all-done.craw = f32[4,8,64,256]{3,2,1,0:T(8,128)} async-done(((f32[4,8,64,256]{3,2,1,0:T(8,128)}), f32[4,8,64,256]{3,2,1,0:T(8,128)}, u32[]{:S(2)}, u32[]{:S(2)}) %all-to-all-start) | async-done | bytes 2097184 | tf_op jit(solution)/shard_map/all_to_all | solution.py:531
  35.2 1.1 fusion.2
  36.2 0.1 collective-permute-start.2
  36.3 0.0 copy-start
  36.3 5.3 %collective-permute-start.3 = (f32[1,256,256]{2,1,0:T(8,128)S(1)}, f32[1,256,256]{2,1,0:T(8,128)S(1)}, u32[]{:S(2)}, u32[]{:S(2)}) collective-permute-start(f32[1,256,256]{2,1,0:T(8,128)S(1)} %bitcast.7), channel_id=1, source_target_pairs={{1,0},{2,1},{3,2},{4,3},{5,4},{6,5},{7,6},{8,7},{9,8},{10,9},{11,1... | collective-permute-start | bytes 786440 | tf_op jit(solution)/shard_map/ppermute | solution.py:495
  41.6 0.0 collective-permute-done.1.uhi
  41.6 0.0 collective-permute-done.ulo
  41.6 4.0 %collective-permute-done.2.clo = f32[1,256,256]{2,1,0:T(8,128)S(1)} collective-permute-done((f32[1,256,256]{2,1,0:T(8,128)S(1)}, f32[1,256,256]{2,1,0:T(8,128)S(1)}, u32[]{:S(2)}, u32[]{:S(2)}) %collective-permute-start.2) | collective-permute-done | bytes 262176 | tf_op jit(solution)/shard_map/ppermute | solution.py:494
  45.7 0.0 collective-permute-done.3.chi
  45.7 0.0 copy-done.1
  45.7 0.0 copy-done.3
  45.7 0.0 copy-done.4
  45.7 7.8 %start.1 = (f32[9,256,256]{2,1,0:T(8,128)S(1)}, f32[8,256,256]{2,1,0:T(8,128)S(1)}, f32[8,256,256]{2,1,0:T(8,128)S(1)}, f32[8,256,256]{2,1,0:T(8,128)S(1)}, f32[...) custom-call(s32[1]{0:T(128)} %bitcast.1.core_ref.refs_0_, ...), custom_call_target="tpu_custom_call" | custom-call | tf_op jit(solution)/shard_map/start/pallas_call | solution.py:470
  53.5 0.0 copy-start.2
  53.5 0.1 collective-permute-start.4
  53.6 1.5 collective-permute-done.4.other
  55.1 0.0 copy-done
  55.1 0.1 join0.1
  55.2 18.4 %all_to_all.50.refs_0_ = f32[16,40,128]{2,1,0:T(8,128)S(1)} all-to-all(f32[16,40,128]{2,1,0:T(8,128)S(1)} %join0.1), channel_id=1, replica_groups={{0,2,4,6,8,10,12,14,16,18,20,22,24,26,28,30},{1,3,5,7,9,11,13,15,17,19,..., dimensions={0} | all-to-all | bytes 655360 | tf_op jit(solution)/shard_map/all_to_all | solution.py:486
  73.6 0.1 scan0.1
  73.7 12.7 %all_to_all.51.carry = f32[16,32,128]{2,1,0:T(8,128)S(1)} all-to-all(f32[16,32,128]{2,1,0:T(8,128)S(1)} %scan0.1), channel_id=1, replica_groups={{0,2,4,6,8,10,12,14,16,18,20,22,24,26,28,30},{1,3,5,7,9,11,13,15,17,19,..., dimensions={0} | all-to-all | bytes 524288 | tf_op jit(solution)/shard_map/all_to_all | solution.py:486
  86.5 0.1 part0.1
  86.5 0.1 collective-permute-start.5
  86.6 1.5 collective-permute-done.5.refs_3_
  88.1 8.4 %step0.1 = (f32[8,256,256]{2,1,0:T(8,128)S(1)}, f32[8,256,256]{2,1,0:T(8,128)S(1)}, f32[8,256,256]{2,1,0:T(8,128)S(1)}, f32[65,8,128]{2,1,0:T(8,128)S(1)}, f32[65,8,128]{2,1,0:T(8,128)S(1)}) custom-call(s32[1]{0:T(128)} %bitcast.1.core_ref.refs_0_, f32[8,256,256]{2,1,0:T(8,128)S(1)} %get-tuple-element.55.refs_1_, ...), custom_call_target="tpu_custom_call" | custom-call | tf_op jit(solution)/shard_map/step0/pallas_call | solution.py:470
  96.6 0.2 collective-permute-start.6
  96.8 1.4 collective-permute-done.6.other
  98.2 0.1 join1.1
  98.3 15.0 %all_to_all.52.refs_0_ = f32[16,40,128]{2,1,0:T(8,128)S(1)} all-to-all(f32[16,40,128]{2,1,0:T(8,128)S(1)} %join1.1), channel_id=1, replica_groups={{0,2,4,6,8,10,12,14,16,18,20,22,24,26,28,30},{1,3,5,7,9,11,13,15,17,19,..., dimensions={0} | all-to-all | bytes 655360 | tf_op jit(solution)/shard_map/all_to_all | solution.py:486
  113.2 0.3 scan1.1
  113.5 12.7 %all_to_all.53.carry = f32[16,32,128]{2,1,0:T(8,128)S(1)} all-to-all(f32[16,32,128]{2,1,0:T(8,128)S(1)} %get-tuple-element.72), channel_id=1, replica_groups={{0,2,4,6,8,10,12,14,16,18,20,22,24,26,28,30},{1,3,5,7,9,11,13,15,17,19,..., dimensions={0} | all-to-all | bytes 524288 | tf_op jit(solution)/shard_map/all_to_all | solution.py:486
  126.2 0.1 part1.1
  126.3 0.1 collective-permute-start.7
  126.4 1.5 collective-permute-done.7.refs_3_
  127.9 9.1 %step1.1 = (f32[8,256,256]{2,1,0:T(8,128)S(1)}, f32[8,256,256]{2,1,0:T(8,128)S(1)}, f32[8,256,256]{2,1,0:T(8,128)S(1)}, f32[8,256,256]{2,1,0:T(8,128)S(1)}, f32[...) custom-call(s32[1]{0:T(128)} %bitcast.1.core_ref.refs_0_, ...), custom_call_target="tpu_custom_call" | custom-call | tf_op jit(solution)/shard_map/step1/pallas_call | solution.py:470
  137.0 0.2 collective-permute-start.8
  137.2 1.4 collective-permute-done.8.other
  138.6 0.1 join2.1
  138.7 15.0 %all_to_all.54.refs_0_ = f32[16,40,128]{2,1,0:T(8,128)S(1)} all-to-all(f32[16,40,128]{2,1,0:T(8,128)S(1)} %join2.1), channel_id=1, replica_groups={{0,2,4,6,8,10,12,14,16,18,20,22,24,26,28,30},{1,3,5,7,9,11,13,15,17,19,..., dimensions={0} | all-to-all | bytes 655360 | tf_op jit(solution)/shard_map/all_to_all | solution.py:486
  153.7 0.3 scan2.1
  153.9 12.7 %all_to_all.55.carry = f32[16,32,128]{2,1,0:T(8,128)S(1)} all-to-all(f32[16,32,128]{2,1,0:T(8,128)S(1)} %get-tuple-element.81), channel_id=1, replica_groups={{0,2,4,6,8,10,12,14,16,18,20,22,24,26,28,30},{1,3,5,7,9,11,13,15,17,19,..., dimensions={0} | all-to-all | bytes 524288 | tf_op jit(solution)/shard_map/all_to_all | solution.py:486
  166.6 0.1 part2.1
  166.7 0.1 collective-permute-start.9
  166.8 1.5 collective-permute-done.9.refs_3_
  168.3 9.6 %step2.1 = (f32[8,256,256]{2,1,0:T(8,128)S(1)}, f32[8,256,256]{2,1,0:T(8,128)S(1)}, f32[8,256,256]{2,1,0:T(8,128)S(1)}, f32[8,256,256]{2,1,0:T(8,128)S(1)}, f32[...) custom-call(s32[1]{0:T(128)} %bitcast.1.core_ref.refs_0_, ...), custom_call_target="tpu_custom_call" | custom-call | tf_op jit(solution)/shard_map/step2/pallas_call | solution.py:470
  177.9 0.2 collective-permute-start.10
  178.1 1.4 collective-permute-done.10.other
  179.5 0.1 join3.1
  179.6 15.0 %all_to_all.56.refs_0_ = f32[16,40,128]{2,1,0:T(8,128)S(1)} all-to-all(f32[16,40,128]{2,1,0:T(8,128)S(1)} %join3.1), channel_id=1, replica_groups={{0,2,4,6,8,10,12,14,16,18,20,22,24,26,28,30},{1,3,5,7,9,11,13,15,17,19,..., dimensions={0} | all-to-all | bytes 655360 | tf_op jit(solution)/shard_map/all_to_all | solution.py:486
  194.6 0.3 scan3.1
  194.8 12.7 %all_to_all.57.carry = f32[16,32,128]{2,1,0:T(8,128)S(1)} all-to-all(f32[16,32,128]{2,1,0:T(8,128)S(1)} %get-tuple-element.93), channel_id=1, replica_groups={{0,2,4,6,8,10,12,14,16,18,20,22,24,26,28,30},{1,3,5,7,9,11,13,15,17,19,..., dimensions={0} | all-to-all | bytes 524288 | tf_op jit(solution)/shard_map/all_to_all | solution.py:486
  207.5 0.1 part3.1
  207.6 0.1 collective-permute-start.11
  207.7 1.5 collective-permute-done.11.refs_3_
  209.2 7.2 %step3.1 = (f32[8,256,256]{2,1,0:T(8,128)S(1)}, f32[32,8,128]{2,1,0:T(8,128)S(1)}) custom-call(s32[1]{0:T(128)} %bitcast.1.core_ref.refs_0_, f32[8,256,256]{2,1,0:T(8,128)S(1)} %get-tuple-element.92.refs_1_, f32[64,8,128]{2,1,0:T(8,128)S(1)} %get-tuple-element.94.refs_2_, f32[64,8,128]{2,1,0:T(8,128)S(1)} %collective-permute-done.11.refs_3_, ...), custom_call_target="tpu_custom_call" | custom-call | tf_op jit(solution)/shard_map/step3/pallas_call | solution.py:470
  216.4 10.5 %all_to_all.58.refs_3_ = f32[32,8,128]{2,1,0:T(8,128)S(1)} all-to-all(f32[32,8,128]{2,1,0:T(8,128)S(1)} %get-tuple-element.102), channel_id=1, replica_groups=mesh['px'=8,'py'=4] {'px','py'}, dimensions={0} | all-to-all | bytes 262144 | tf_op jit(solution)/shard_map/all_to_all | solution.py:486
  226.9 2.2 finish.1
  (7 shorter events, 0.0 us)
Async XLA Ops:
  1.5 33.7 %all-to-all-start = ((f32[4,8,64,256]{3,2,1,0:T(8,128)}), f32[4,8,64,256]{3,2,1,0:T(8,128)}, u32[]{:S(2)}, u32[]{:S(2)}) async-start(f32[4,8,64,256]{3,2,1,0:T(8,128)} %bitcast.6), calls=%async_computation | async-start | bytes 4194304 | tf_op jit(solution)/shard_map/all_to_all | solution.py:531
  10.5 35.2 %copy-start.1 = (f32[256,256]{1,0:T(8,128)S(1)}, f32[256,256]{1,0:T(8,128)}, u32[]{:S(2)}) copy-start(f32[256,256]{1,0:T(8,128)} %constant.106.clone.rho.refs_4_) | copy-start | bytes 786436
  10.5 35.2 %copy-start.3 = (bf16[256,256]{1,0:T(8,128)(2,1)S(1)}, bf16[256,256]{1,0:T(8,128)(2,1)}, u32[]{:S(2)}) copy-start(bf16[256,256]{1,0:T(8,128)(2,1)} %constant.109.clone.hl.refs_7_) | copy-start | bytes 393220
  10.5 35.2 %copy-start.4 = (bf16[256,256]{1,0:T(8,128)(2,1)S(1)}, bf16[256,256]{1,0:T(8,128)(2,1)}, u32[]{:S(2)}) copy-start(bf16[256,256]{1,0:T(8,128)(2,1)} %constant.108.clone.hh.refs_6_) | copy-start | bytes 393220
  11.2 30.4 %collective-permute-start.1 = (f32[1,256,256]{2,1,0:T(8,128)}, f32[1,256,256]{2,1,0:T(8,128)S(1)}, u32[]{:S(2)}, u32[]{:S(2)}) collective-permute-start(f32[1,256,256]{2,1,0:T(8,128)} %get-tuple-element.108), channel_id=1, source_target_pairs={{1,0},{2,1},{3,2},{4,3},{5,4},{6,5},{7,6},{8,7},{9,8},{10,9},{11,1... | collective-permute-start | bytes 786440 | tf_op jit(solution)/shard_map/ppermute | solution.py:495
  18.3 23.3 %collective-permute-start = (f32[1,256,256]{2,1,0:T(8,128)S(1)}, f32[1,256,256]{2,1,0:T(8,128)S(1)}, u32[]{:S(2)}, u32[]{:S(2)}) collective-permute-start(f32[1,256,256]{2,1,0:T(8,128)S(1)} %get-tuple-element.109), channel_id=1, source_target_pairs={{0,1},{1,2},{2,3},{3,4},{4,5},{5,6},{6,7},{7,8},{8,9},{9,10},{10,1... | collective-permute-start | bytes 786440 | tf_op jit(solution)/shard_map/ppermute | solution.py:494
  36.2 9.4 %collective-permute-start.2 = (f32[1,256,256]{2,1,0:T(8,128)S(1)}, f32[1,256,256]{2,1,0:T(8,128)S(1)}, u32[]{:S(2)}, u32[]{:S(2)}) collective-permute-start(f32[1,256,256]{2,1,0:T(8,128)S(1)} %bitcast.8), channel_id=1, source_target_pairs={{0,1},{1,2},{2,3},{3,4},{4,5},{5,6},{6,7},{7,8},{8,9},{9,10},{10,1... | collective-permute-start | bytes 786440 | tf_op jit(solution)/shard_map/ppermute | solution.py:494
  36.3 18.8 %copy-start = (f32[256,256]{1,0:T(8,128)S(1)}, f32[256,256]{1,0:T(8,128)}, u32[]{:S(2)}) copy-start(f32[256,256]{1,0:T(8,128)} %constant.103.clone.block) | copy-start | bytes 786436
  36.3 9.4 %collective-permute-start.3 = (f32[1,256,256]{2,1,0:T(8,128)S(1)}, f32[1,256,256]{2,1,0:T(8,128)S(1)}, u32[]{:S(2)}, u32[]{:S(2)}) collective-permute-start(f32[1,256,256]{2,1,0:T(8,128)S(1)} %bitcast.7), channel_id=1, source_target_pairs={{1,0},{2,1},{3,2},{4,3},{5,4},{6,5},{7,6},{8,7},{9,8},{10,9},{11,1... | collective-permute-start | bytes 786440 | tf_op jit(solution)/shard_map/ppermute | solution.py:495
  53.5 34.6 %copy-start.2 = (f32[256,256]{1,0:T(8,128)S(1)}, f32[256,256]{1,0:T(8,128)}, u32[]{:S(2)}) copy-start(f32[256,256]{1,0:T(8,128)} %constant.107.clone.refs_5_) | copy-start | bytes 786436
  53.5 1.6 collective-permute-start.4
  86.5 1.6 collective-permute-start.5
  96.6 1.6 collective-permute-start.6
  126.3 1.6 collective-permute-start.7
  137.0 1.6 collective-permute-start.8
  166.7 1.6 collective-permute-start.9
  177.9 1.6 collective-permute-start.10
  207.6 1.6 collective-permute-start.11
